TPU v7x, 32 devices: a whole 2x2x4 slice. The times are simulated.
32 devices in a mesh: grid: 8 (over y, x, core), atom: 4 (over z).
Axes of the slice: x: 2, y: 2, z: 4, core: 2. Of those that a mesh axis runs over, the one named last changes fastest.
Arguments:
- basis_values: bfloat16 [64, 128, 512], P(('grid', 'atom')), may hold values from -8 to 8
- block_lists: int32 [64, 4], P('grid'), may hold values from 0 to 95, as said below
- orbitals: bfloat16 [12288, 4096], P('grid', 'atom'), may hold values from -0.00390625 to 0.00390625
- point_weights: float32 [8192], P(('grid', 'atom')), may hold values from 0.1 to 1
- point_atoms: int32 [8192], P(('grid', 'atom')), may hold values from 0 to 127, as said below
- embed_scale: float32 [256], replicated, may hold values from -4 to 4
- embed_shift: float32 [256], replicated, may hold values from -3 to 3
- message_weight: bfloat16 [2, 256, 256], replicated, may hold values from -0.375 to 0.375
- atom_weight: bfloat16 [2, 256, 256], replicated, may hold values from -0.375 to 0.375
- head_weight: float32 [256], replicated, may hold values from -0.375 to 0.375
Outputs:
- fock_orbitals: float32 [12288, 4096], P('grid', 'atom')
- potential: float32 [8192], P(('grid', 'atom'))
Inputs may be any that keep to these rules, and one draw needn't show every extreme that they name: `block_lists`: each row names 4 different blocks; a batch b of group g = b // 8 names only blocks (g - 1) * 12 to (g + 2) * 12 - 1. `point_atoms`: the 256 points of one device name atom centres of one run of max(8, 1) consecutive centres, counted round.
All inputs are finite; a program needn't handle non-finite values.
Results may differ from a plain program's by a relative error of at most 0.04.
Values may be sent and summed in bfloat16 or wider, within the bound.
A program may use at most 128 MiB of HBM per device.

v0:
```python
import jax
import jax.numpy as jnp
from jax import lax
from jax.sharding import PartitionSpec as P

ATOM_DEV = 32


def padded(cells, sides, width):
    for axis, dim in sides:
        count = lax.axis_size(axis)
        ends = count - 1
        head = lax.slice_in_dim(cells, 0, width, axis=dim)
        tail = lax.slice_in_dim(cells, cells.shape[dim] - width, cells.shape[dim], axis=dim)
        cells = jnp.concatenate(
            [
                lax.ppermute(tail, axis, [(i, (i + 1) % count) for i in range(ends)]),
                cells,
                lax.ppermute(head, axis, [((i + 1) % count, i) for i in range(ends)]),
            ],
            axis=dim,
        )
    return cells


def passed_along(value, axis, steps):
    count = lax.axis_size(axis)
    leading, last = (max(0, -steps), min(count, count - steps))
    return lax.ppermute(value, axis, [(source, source + steps) for source in range(leading, last)])


def orbital_values(piece, lists, blocks):
    count = piece.shape[0]
    chosen = blocks[lists].reshape(count, -1, blocks.shape[2])
    values = jnp.einsum("bpk,bko->bpo", piece, chosen, preferred_element_type=jnp.float32)
    return values.astype(jnp.bfloat16)


def fock_terms(piece, lists, psi_rows, scale_rows, total):
    weighted_psi = (scale_rows[:, :, None] * psi_rows.astype(jnp.float32)).astype(jnp.bfloat16)
    terms = jnp.einsum("bpk,bpo->bko", piece, weighted_psi, preferred_element_type=jnp.float32)
    terms = terms.reshape(-1, total.shape[1], total.shape[2])
    return total.at[lists.reshape(-1)].add(terms)


def atom_update(rows, mass, weight):
    mean = rows / (1.0 + mass[:, None])
    return jax.nn.silu(
        jnp.dot(mean.astype(jnp.bfloat16), weight, preferred_element_type=jnp.float32)
    ).astype(jnp.bfloat16)


def local(
    basis_values,
    block_lists,
    orbitals,
    point_weights,
    point_atoms,
    embed_scale,
    embed_shift,
    message_weight,
    atom_weight,
    head_weight,
):
    own_rows = orbitals.shape[0]
    gathered = padded(orbitals, (("grid", 0),), own_rows)
    width = basis_values.shape[2] // block_lists.shape[1]
    owned = own_rows // width
    blocks = gathered.reshape(-1, width, gathered.shape[1])
    offset = (lax.axis_index("grid") - 1) * owned
    local_lists = block_lists - offset
    group_values = lax.all_gather(basis_values, "atom", axis=0, tiled=True)
    psi = orbital_values(group_values, local_lists, blocks)
    squares = 2.0 * jnp.sum(jnp.square(psi.astype(jnp.float32)), axis=2).reshape(-1)
    density = lax.psum_scatter(squares, "atom", scatter_dimension=0, tiled=True)
    radius = jnp.cbrt(density)
    hidden = jax.nn.silu(radius[:, None] * embed_scale[None, :] + embed_shift[None, :])
    atom_total = ATOM_DEV * lax.axis_size("atom")
    onehot = point_atoms[:, None] == jnp.arange(atom_total, dtype=jnp.int32)[None, :]
    selector = onehot.astype(jnp.bfloat16)
    counts = jnp.dot(point_weights, onehot.astype(jnp.float32), precision=lax.Precision.HIGHEST)
    for layer in range(message_weight.shape[0]):
        message = jax.nn.silu(
            jnp.dot(
                hidden.astype(jnp.bfloat16),
                message_weight[layer],
                preferred_element_type=jnp.float32,
            )
        )
        weighted = (point_weights[:, None] * message).astype(jnp.bfloat16)
        partial_value = lax.dot_general(
            selector, weighted, (((0,), (0,)), ((), ())), preferred_element_type=jnp.float32
        )
        rows, mass = (
            lax.psum_scatter(
                partial_value.astype(jnp.bfloat16), "atom", scatter_dimension=0, tiled=True
            ).astype(jnp.float32),
            lax.psum_scatter(
                counts.astype(jnp.bfloat16), "atom", scatter_dimension=0, tiled=True
            ).astype(jnp.float32),
        )
        rows, mass = (
            lax.psum(rows.astype(jnp.bfloat16), "grid").astype(jnp.float32),
            lax.psum(mass.astype(jnp.bfloat16), "grid").astype(jnp.float32),
        )
        update = atom_update(rows, mass, atom_weight[layer])
        features = lax.all_gather(update, "atom", axis=0, tiled=True)
        picked = jnp.dot(selector, features, preferred_element_type=jnp.float32)
        hidden = hidden + message * picked
    score = jnp.dot(hidden, head_weight, precision=lax.Precision.HIGHEST)
    potential = radius * (1.0 + jnp.tanh(score))
    scaled = lax.all_gather(point_weights * potential, "atom", axis=0, tiled=True)
    scaled = scaled.reshape(psi.shape[0], psi.shape[1])
    empty = jnp.zeros((blocks.shape[0], width, psi.shape[2]), jnp.float32)
    total = fock_terms(group_values, local_lists, psi, scaled, empty)
    rounded = lax.optimization_barrier(
        total.reshape(3, own_rows, total.shape[2]).astype(jnp.bfloat16)
    )
    from_below = passed_along(rounded[2], "grid", 1)
    from_above = passed_along(rounded[0], "grid", -1)
    fock_orbitals = (
        rounded[1].astype(jnp.float32)
        + from_below.astype(jnp.float32)
        + from_above.astype(jnp.float32)
    )
    return (fock_orbitals, potential)


def solution(mesh):
    return jax.shard_map(
        local,
        mesh=mesh,
        in_specs=(
            P(("grid", "atom"), None, None),
            P("grid", None),
            P("grid", "atom"),
            P(("grid", "atom")),
            P(("grid", "atom")),
            P(),
            P(),
            P(),
            P(),
            P(),
        ),
        out_specs=(P("grid", "atom"), P(("grid", "atom"))),
        check_vma=False,
    )
```

profile of v0, /device:TPU:4, one launch (start us, length us, event | category | flops | bytes accessed | tf_op | source)
XLA Modules:
  0.0 382.2 jit_solution(17801122140071858288)
XLA Ops:
  7.2 1.9 collective-permute-start
  9.2 4.5 %collective-permute-start.1 = (bf16[1536,1024]{1,0:T(8,128)(2,1)}, bf16[1536,1024]{1,0:T(8,128)(2,1)}, u32[]{:S(2)}, u32[]{:S(2)}) collective-permute-start(bf16[1536,1024]{1,0:T(8,128)(2,1)} %param.12), channel_id=1, source_target_pairs={{4,0},{8,4},{12,8},{16,12},{20,16},{24,20},{28,24},{5,1},{9,5},{13... | collective-permute-start | bytes 9437192 | tf_op jit(solution)/shard_map/ppermute | solution.py:19
  13.8 1.2 dynamic-slice
  17.4 60.5 %collective-permute-done = bf16[1536,1024]{1,0:T(8,128)(2,1)S(1)} collective-permute-done((bf16[1536,1024]{1,0:T(8,128)(2,1)}, bf16[1536,1024]{1,0:T(8,128)(2,1)S(1)}, u32[]{:S(2)}, u32[]{:S(2)}) %collective-permute-start) | collective-permute-done | bytes 3145760 | tf_op jit(solution)/shard_map/ppermute | solution.py:17
  77.9 1.0 collective-permute-done.1
  78.8 7.0 %pad_maximum_fusion = bf16[4608,1024]{1,0:T(8,128)(2,1)} fusion(bf16[1536,1024]{1,0:T(8,128)(2,1)} %collective-permute-done.1, bf16[1536,1024]{1,0:T(8,128)(2,1)} %param.12, bf16[1536,1024]{1,0:T(8,128)(2,1)S(1)} %collective-permute-done), kind=kLoop, calls=%fused_computation.2 | loop fusion | flops 28311552 | bytes 18874368 | tf_op jit(solution)/shard_map/concatenate | solution.py:15
  85.8 8.7 %gather_fusion = bf16[32,128,1024]{2,1,0:T(8,128)(2,1)} fusion(bf16[36,128,1024]{2,1,0:T(8,128)(2,1)} %bitcast.59, s32[1024]{0:T(1024)S(1)} %pad_clamp_fusion), kind=kCustom, calls=%fused_computation | custom fusion | bytes 16777344 | tf_op jit(solution)/shard_map/gather | solution.py:34
  94.6 6.4 %fusion.1 = (f32[8,128]{1,0:T(8,128)S(1)}, bf16[8,1024,128]{2,1,0:T(8,128)(2,1)S(1)}) fusion(bf16[8,512,1024]{2,1,0:T(8,128)(2,1)} %bitcast.60, bf16[8,128,512]{2,1,0:T(8,128)(2,1)} %all-gather.3.cloned.1.call-done), kind=kOutput, calls=%fused_computation.7 | convolution fusion | flops 1077935104 | bytes 11538432 | tf_op jit(solution)/shard_map/bpk,bko->bpo/dot_general | solution.py:35
  101.1 12.1 %all-reduce = f32[1024]{0:T(1024)S(1)} all-reduce(f32[1024]{0:T(1024)S(1)} %multiply_bitcast_fusion), channel_id=2, replica_groups=mesh['grid'=8,'atom'=4] {'atom'}, use_global_device_ids=true, to_apply=%region_1.0.clone | all-reduce | flops 1024 | bytes 8192
  113.3 1.2 divide_multiply_fusion.1
  114.5 0.9 convolution_convert_fusion.2
  115.7 8.4 %all-reduce.1 = bf16[128]{0:T(256)(128)(2,1)S(1)} all-reduce(bf16[128]{0:T(256)(128)(2,1)S(1)} %fusion.8), channel_id=4, replica_groups=mesh['grid'=8,'atom'=4] {'atom'}, use_global_device_ids=true, to_apply=%region_4.5.clone | all-reduce | flops 128 | bytes 512
  124.2 8.0 %reduce-scatter.3.cloned.1.call-done = bf16[32,256]{1,0:T(8,128)(2,1)} async-done(((bf16[128,256]{1,0:T(8,128)(2,1)}), bf16[32,256]{1,0:T(8,128)(2,1)}) %reduce-scatter.3.cloned.1.call-update) | async-done | bytes 16400 | tf_op jit(solution)/shard_map/reduce_scatter | solution.py:95
  132.1 22.9 %all-reduce.2 = (bf16[32,256]{1,0:T(8,128)(2,1)S(1)}, bf16[32]{0:T(256)(128)(2,1)S(1)}) all-reduce(bf16[32,256]{1,0:T(8,128)(2,1)} %reduce-scatter.3.cloned.1.call-done, bf16[32]{0:T(256)(128)(2,1)S(1)} %dynamic-slice.3), channel_id=1, replica_groups=mesh['grid'=8,'atom'=4] {'grid'}, use_global_device_ids=true, to_apply=%region_3.4 | all-reduce | flops 8224 | bytes 32896 | tf_op jit(solution)/shard_map/psum | solution.py:103
  155.0 1.1 multiply_convert_fusion.5
  156.2 13.1 %all_gather.13 = bf16[128,256]{1,0:T(8,128)(2,1)S(1)} all-gather(bf16[32,256]{1,0:T(8,128)(2,1)S(1)} %multiply_convert_fusion.5), channel_id=1, replica_groups=mesh['grid'=8,'atom'=4] {'atom'}, dimensions={0}, use_global_device_ids=true | all-gather | bytes 81920 | tf_op jit(solution)/shard_map/all_gather | solution.py:107
  170.2 1.1 divide_multiply_fusion
  171.4 0.9 convolution_convert_fusion.1
  172.3 16.7 %reduce-scatter.5.cloned.1.call-done = bf16[32,256]{1,0:T(8,128)(2,1)} async-done(((bf16[128,256]{1,0:T(8,128)(2,1)}), bf16[32,256]{1,0:T(8,128)(2,1)}) %reduce-scatter.5.cloned.1.call-update) | async-done | bytes 16400 | tf_op jit(solution)/shard_map/reduce_scatter | solution.py:95
  189.1 22.9 %psum.26 = bf16[32,256]{1,0:T(8,128)(2,1)S(1)} all-reduce(bf16[32,256]{1,0:T(8,128)(2,1)} %reduce-scatter.5.cloned.1.call-done), channel_id=1, replica_groups=mesh['grid'=8,'atom'=4] {'grid'}, use_global_device_ids=true, to_apply=%region_7.8 | all-reduce | flops 8192 | bytes 32768 | tf_op jit(solution)/shard_map/psum | solution.py:103
  212.0 1.1 multiply_convert_fusion.4
  213.1 13.1 %all_gather.14 = bf16[128,256]{1,0:T(8,128)(2,1)S(1)} all-gather(bf16[32,256]{1,0:T(8,128)(2,1)S(1)} %multiply_convert_fusion.4), channel_id=1, replica_groups=mesh['grid'=8,'atom'=4] {'atom'}, dimensions={0}, use_global_device_ids=true | all-gather | bytes 81920 | tf_op jit(solution)/shard_map/all_gather | solution.py:107
  226.2 1.2 fusion.6
  228.4 8.3 %all-gather = f32[4,1,256]{2,1,0:T(1,128)S(1)} all-gather(f32[1,1,256]{2,1,0:T(1,128)S(1)} %bitcast.64), channel_id=1, replica_groups=mesh['grid'=8,'atom'=4] {'atom'}, dimensions={0}, use_global_device_ids=true | all-gather | bytes 5120 | tf_op jit(solution)/shard_map/all_gather | solution.py:112
  236.7 8.1 %fusion.3 = f32[8,1024,512]{1,2,0:T(8,128)} fusion(bf16[8,128,512]{2,1,0:T(8,128)(2,1)S(1)} %copy-done.2, bf16[8,1024,128]{2,1,0:T(8,128)(2,1)S(1)} %get-tuple-element.11, f32[8,128]{1,0:T(8,128)S(1)} %bitcast.61), kind=kOutput, calls=%fused_computation.12 | convolution fusion | flops 1076887552 | bytes 19927040 | tf_op jit(solution)/shard_map/bpk,bpo->bko/dot_general | solution.py:41
  244.9 8.9 %broadcast_in_dim.4 = f32[36,128,1024]{2,1,0:T(8,128)} broadcast(f32[]{:T(128)} %constant.9.clone.1), dimensions={} | broadcast | bytes 18874372 | tf_op jit(solution)/shard_map/broadcast_in_dim | solution.py:114
  253.7 36.2 %scatter_fusion = f32[36,128,1024]{2,1,0:T(8,128)} fusion(f32[36,128,1024]{2,1,0:T(8,128)} %broadcast_in_dim.4, s32[32]{0:T(128)S(1)} %fusion.45, f32[32,128,1024]{2,1,0:T(8,128)} %bitcast.56), kind=kCustom, calls=%fused_computation.1 | custom fusion | flops 4194304 | bytes 50331776 | tf_op jit(solution)/shard_map/scatter-add | solution.py:43
  289.9 7.1 %convert_element_type.102 = bf16[36,128,1024]{2,1,0:T(8,128)(2,1)S(1)} convert(f32[36,128,1024]{2,1,0:T(8,128)} %scatter_fusion) | non-fusion elementwise | flops 4718592 | bytes 28311552 | tf_op jit(solution)/shard_map/convert_element_type | solution.py:117
  297.8 1.9 collective-permute-start.2
  299.7 4.5 %collective-permute-start.3 = (bf16[1536,1024]{1,0:T(8,128)(2,1)S(1)}, bf16[1536,1024]{1,0:T(8,128)(2,1)S(1)}, u32[]{:S(2)}, u32[]{:S(2)}) collective-permute-start(bf16[1536,1024]{1,0:T(8,128)(2,1)S(1)} %get-tuple-element.9), channel_id=1, source_target_pairs={{4,0},{8,4},{12,8},{16,12},{20,16},{24,20},{28,24},{5,1},{9,5},{13... | collective-permute-start | bytes 9437192 | tf_op jit(solution)/shard_map/ppermute | solution.py:29
  304.3 66.5 %collective-permute-done.2 = bf16[1536,1024]{1,0:T(8,128)(2,1)S(1)} collective-permute-done((bf16[1536,1024]{1,0:T(8,128)(2,1)S(1)}, bf16[1536,1024]{1,0:T(8,128)(2,1)S(1)}, u32[]{:S(2)}, u32[]{:S(2)}) %collective-permute-start.2) | collective-permute-done | bytes 3145760 | tf_op jit(solution)/shard_map/ppermute | solution.py:29
  370.8 4.9 %fusion = f32[1536,1024]{1,0:T(8,128)} fusion(bf16[1536,1024]{1,0:T(8,128)(2,1)S(1)} %collective-permute-done.3, bf16[1536,1024]{1,0:T(8,128)(2,1)S(1)} %collective-permute-done.2, bf16[3,1536,1024]{2,1,0:T(8,128)(2,1)S(1)} %bitcast.58), kind=kLoop, calls=%fused_computation.4 | loop fusion | flops 7864320 | bytes 15728640 | tf_op jit(solution)/shard_map/add | solution.py:122
  (40 shorter events, 4.3 us)
Async XLA Ops:
  7.2 220.2 %copy-start = (f32[256]{0:T(256)S(1)}, f32[256]{0:T(256)}, u32[]{:S(2)}) copy-start(f32[256]{0:T(256)} %param.19) | copy-start | bytes 3076
  7.2 87.4 %all-gather.3.cloned.1.call-start = ((), (), s32[]{:S(2)}) async-start(), calls=%async_computation.2 | async-start | bytes 1310720 | tf_op jit(solution)/shard_map/all_gather | solution.py:72
  7.2 70.7 %collective-permute-start = (bf16[1536,1024]{1,0:T(8,128)(2,1)}, bf16[1536,1024]{1,0:T(8,128)(2,1)S(1)}, u32[]{:S(2)}, u32[]{:S(2)}) collective-permute-start(bf16[1536,1024]{1,0:T(8,128)(2,1)} %param.12), channel_id=1, source_target_pairs={{0,4},{4,8},{8,12},{12,16},{16,20},{20,24},{24,28},{1,5},{5,9},{9,... | collective-permute-start | bytes 9437192 | tf_op jit(solution)/shard_map/ppermute | solution.py:17
  9.2 69.7 %collective-permute-start.1 = (bf16[1536,1024]{1,0:T(8,128)(2,1)}, bf16[1536,1024]{1,0:T(8,128)(2,1)}, u32[]{:S(2)}, u32[]{:S(2)}) collective-permute-start(bf16[1536,1024]{1,0:T(8,128)(2,1)} %param.12), channel_id=1, source_target_pairs={{4,0},{8,4},{12,8},{16,12},{20,16},{24,20},{28,24},{5,1},{9,5},{13... | collective-permute-start | bytes 9437192 | tf_op jit(solution)/shard_map/ppermute | solution.py:19
  13.7 118.4 %reduce-scatter.3.cloned.1.call-start = ((), (), s32[]{:S(2)}) async-start(), calls=%async_computation.3 | async-start | bytes 81920 | tf_op jit(solution)/shard_map/reduce_scatter | solution.py:95
  94.6 18.7 %copy-start.6 = (f32[256]{0:T(256)S(1)}, f32[256]{0:T(256)}, u32[]{:S(2)}) copy-start(f32[256]{0:T(256)} %param.16) | copy-start | bytes 3076
  94.6 18.7 %copy-start.7 = (f32[256]{0:T(256)S(1)}, f32[256]{0:T(256)}, u32[]{:S(2)}) copy-start(f32[256]{0:T(256)} %param.15) | copy-start | bytes 3076
  94.6 19.9 %copy-start.4 = (s32[256]{0:T(256)S(1)}, s32[256]{0:T(256)}, u32[]{:S(2)}) copy-start(s32[256]{0:T(256)} %param.14) | copy-start | bytes 3076
  94.6 19.9 %copy-start.5 = (f32[256]{0:T(256)S(1)}, f32[256]{0:T(256)}, u32[]{:S(2)}) copy-start(f32[256]{0:T(256)} %param.13) | copy-start | bytes 3076
  101.0 135.7 %copy-start.2 = (bf16[8,128,512]{2,1,0:T(8,128)(2,1)S(1)}, bf16[8,128,512]{2,1,0:T(8,128)(2,1)}, u32[]{:S(2)}) copy-start(bf16[8,128,512]{2,1,0:T(8,128)(2,1)} %all-gather.3.cloned.1.call-done) | copy-start | bytes 3145732
  115.5 73.6 %reduce-scatter.5.cloned.1.call-start = ((), (), s32[]{:S(2)}) async-start(), calls=%async_computation.4 | async-start | bytes 81920 | tf_op jit(solution)/shard_map/reduce_scatter | solution.py:95
  169.5 0.7 copy-start.3
  297.8 73.0 %collective-permute-start.2 = (bf16[1536,1024]{1,0:T(8,128)(2,1)S(1)}, bf16[1536,1024]{1,0:T(8,128)(2,1)S(1)}, u32[]{:S(2)}, u32[]{:S(2)}) collective-permute-start(bf16[1536,1024]{1,0:T(8,128)(2,1)S(1)} %get-tuple-element.8), channel_id=1, source_target_pairs={{0,4},{4,8},{8,12},{12,16},{16,20},{20,24},{24,28},{1,5},{5,9},{9,... | collective-permute-start | bytes 9437192 | tf_op jit(solution)/shard_map/ppermute | solution.py:29
  299.7 76.0 %copy-start.1 = (f32[256]{0:T(256)S(1)}, f32[256]{0:T(256)}, u32[]{:S(2)}) copy-start(f32[256]{0:T(256)} %param.19) | copy-start | bytes 3076
  299.7 71.0 %collective-permute-start.3 = (bf16[1536,1024]{1,0:T(8,128)(2,1)S(1)}, bf16[1536,1024]{1,0:T(8,128)(2,1)S(1)}, u32[]{:S(2)}, u32[]{:S(2)}) collective-permute-start(bf16[1536,1024]{1,0:T(8,128)(2,1)S(1)} %get-tuple-element.9), channel_id=1, source_target_pairs={{4,0},{8,4},{12,8},{16,12},{20,16},{24,20},{28,24},{5,1},{9,5},{13... | collective-permute-start | bytes 9437192 | tf_op jit(solution)/shard_map/ppermute | solution.py:29
Sparse Core Ops, SparseCore 0:
  13.9 28.3 all-gather.2
  115.6 16.5 reduce-scatter.2
  172.4 16.5 reduce-scatter.4
where the time goes:
time: 384 us; the launch traced here: 382 us
  waiting for transfers between devices  153 us (40%)
  blocking collectives  101 us (26%)
  other arithmetic  56.6 us (15%)
  matrix products  22.9 us (6%)
  local copies, waits for them, and re-layouts  20.8 us (5%)
  between operations  15.3 us (4%)
  starting transfers between devices  13.1 us (3%)
    ppermute x2, waiting for transfers between devices, passed_along(): lax.ppermute(value, axis, [(source, source + steps) for source in range(l...  66.5 us
    ppermute x1, waiting for transfers between devices, padded(): lax.ppermute(tail, axis, [(i, (i + 1) % count) for i in range(ends)])  60.5 us
    psum x2, blocking collectives, local(): lax.psum(rows.astype(jnp.bfloat16), 'grid').astype(jnp.float32)  45.8 us
    scatter-add x1, other arithmetic, fock_terms(): return total.at[lists.reshape(-1)].add(terms)  36.2 us
    all_gather x2, blocking collectives, local(): features = lax.all_gather(update, 'atom', axis=0, tiled=True)  26.3 us
    reduce_scatter x2, waiting for transfers between devices, local(): lax.psum_scatter(partial_value.astype(jnp.bfloat16), 'atom', scatter_dime...  24.7 us
    unnamed x2, blocking collectives  20.5 us
    broadcast_in_dim x1, local copies, waits for them, and re-layouts, local(): empty = jnp.zeros((blocks.shape[0], width, psi.shape[2]), jnp.float32)  8.87 us
  transfers between devices with their start and end apart: 7, of which 5 were waited for; matrix products, arithmetic and copies ran while one was open for 5% of the time, Pallas kernels for 0%

commit v1 on v0

v1 whole, which is shorter than its diff:
```python
import functools
import jax
import jax.numpy as jnp
from jax import lax
from jax.experimental import pallas as pl
from jax.experimental.pallas import tpu as pltpu
from jax.sharding import PartitionSpec as P

ATOM_DEV = 32
RUN = max(ATOM_DEV // 4, 1)
LANES = 128
VMEM = pl.BlockSpec(memory_space=pltpu.VMEM)
MESH = pl.DeviceIdType.MESH


def passed_along(value, axis, steps):
    count = lax.axis_size(axis)
    leading, last = (max(0, -steps), min(count, count - steps))
    return lax.ppermute(value, axis, [(source, source + steps) for source in range(leading, last)])


def to_columns(rows):
    parts = [
        jnp.transpose(jnp.broadcast_to(rows[i : i + 1, :], (LANES, LANES)))
        for i in range(rows.shape[0])
    ]
    return jnp.concatenate(parts, axis=0)


def to_rows(columns):
    parts = []
    for i in range(columns.shape[0] // LANES):
        piece = jnp.broadcast_to(columns[i * LANES : (i + 1) * LANES, :], (LANES, LANES))
        parts.append(jnp.transpose(piece)[0:1, :])
    return jnp.concatenate(parts, axis=0)


def psi_kernel(lists, basis, below, own, above, psi, dens, rows, sums):
    step = pl.program_id(0)
    owned = own.shape[0]
    rows[0:owned, :] = below[...]
    rows[owned : 2 * owned, :] = own[...]
    rows[2 * owned : 3 * owned, :] = above[...]
    count, points, depth = basis.shape
    picks = lists.shape[1]
    width = depth // picks
    wide = psi.shape[2]

    @pl.when(step == 0)
    def _():
        sums[...] = jnp.zeros_like(sums)

    @pl.loop(0, count)
    def _(b):
        chosen = jnp.concatenate(
            [
                rows[pl.ds(pl.multiple_of(lists[b, j] * width, width), width), :]
                for j in range(picks)
            ],
            axis=0,
        )
        value = jnp.dot(basis[b], chosen, preferred_element_type=jnp.float32)
        rounded = value.astype(jnp.bfloat16)
        psi[b] = rounded
        square = jnp.square(rounded.astype(jnp.float32))
        total = square[:, 0:LANES]
        for i in range(1, wide // LANES):
            total = total + square[:, i * LANES : (i + 1) * LANES]
        sums[b] += total

    @pl.when(step == pl.num_programs(0) - 1)
    def _():
        for b in range(count):
            dens[b : b + 1, :] = jnp.sum(jnp.transpose(sums[b]), axis=0, keepdims=True)


def psi_and_density(lists, basis, below, own, above):
    owned, columns = own.shape
    count, points, depth = basis.shape
    wide = min(columns, 256)
    tile = pl.BlockSpec((owned, wide), lambda i, lists: (0, i))
    return pl.pallas_call(
        psi_kernel,
        out_shape=(
            jax.ShapeDtypeStruct((count, points, columns), jnp.bfloat16),
            jax.ShapeDtypeStruct((count, points), jnp.float32),
        ),
        grid_spec=pltpu.PrefetchScalarGridSpec(
            num_scalar_prefetch=1,
            grid=(columns // wide,),
            in_specs=[
                pl.BlockSpec((count, points, depth), lambda i, lists: (0, 0, 0)),
                tile,
                tile,
                tile,
            ],
            out_specs=(
                pl.BlockSpec((count, points, wide), lambda i, lists: (0, 0, i)),
                pl.BlockSpec((count, points), lambda i, lists: (0, 0)),
            ),
            scratch_shapes=[
                pltpu.VMEM((3 * owned, wide), jnp.bfloat16),
                pltpu.VMEM((count, points, LANES), jnp.float32),
            ],
        ),
        compiler_params=pltpu.CompilerParams(vmem_limit_bytes=48 << 20),
        cost_estimate=pl.CostEstimate(
            flops=2 * count * points * depth * columns,
            bytes_accessed=8 * owned * columns,
            transcendentals=0,
        ),
        name="psi_and_density",
    )(lists, basis, below, own, above)


def potential_kernel(
    shape, layers, dens, info, mine, hot, hot_t, weights, scale, shift, mw, aw, head,
    pot, near, dens_buf, info_buf, rows_out, rows_buf, scaled_out, scaled_buf, sent, got,
):
    n_grid, n_atom = shape
    n = n_grid * n_atom
    grid, atom = lax.axis_index("grid"), lax.axis_index("atom")
    me = grid * n_atom + atom

    def other(d):
        t = lax.rem(me + d, n)
        return (t // n_atom, lax.rem(t, n_atom))

    def to_all(source, held, k):
        @pl.loop(1, n)
        def _(d):
            pltpu.make_async_remote_copy(
                src_ref=source,
                dst_ref=held.at[me],
                send_sem=sent.at[k],
                recv_sem=got.at[k],
                device_id=other(d),
                device_id_type=MESH,
            ).start()

    def wait_all(held, sem, count):
        part = held.at[pl.ds(0, count)]
        pltpu.make_async_copy(part, part, sem).wait()

    barrier = pltpu.get_barrier_semaphore()

    @pl.loop(1, n)
    def _(d):
        pl.semaphore_signal(barrier, inc=1, device_id=other(d), device_id_type=MESH)

    pl.semaphore_wait(barrier, n - 1)

    @pl.loop(1, n_atom)
    def _(d):
        to = lax.rem(atom + d, n_atom)
        pltpu.make_async_remote_copy(
            src_ref=dens.at[to],
            dst_ref=dens_buf.at[atom],
            send_sem=sent.at[0],
            recv_sem=got.at[0],
            device_id=(grid, to),
            device_id_type=MESH,
        ).start()

    to_all(info, info_buf, 1)
    dens_buf[atom] = dens[atom]
    info_buf[me] = info[...]
    weight = to_columns(weights[...])[:, 0:1]

    wait_all(dens_buf, got.at[0], n_atom - 1)
    density = to_columns(2.0 * jnp.sum(dens_buf[...], axis=0))
    safe = jnp.where(density > 0.0, density, 1.0)
    radius = jnp.where(density > 0.0, jnp.exp(jnp.log(safe) * (1.0 / 3.0)), 0.0)[:, 0:1]
    hidden = jax.nn.silu(radius * scale[...] + shift[...])
    halves = hidden.shape[1] // LANES
    picks = []
    share = None
    for layer in range(layers):
        message = jax.nn.silu(
            jnp.dot(hidden.astype(jnp.bfloat16), mw[layer], preferred_element_type=jnp.float32)
        )
        weighted = (weight * message).astype(jnp.bfloat16)
        part = jnp.dot(hot_t[...], weighted, preferred_element_type=jnp.float32)
        rows_out[layer] = jnp.concatenate(
            [part[0:RUN, h * LANES : (h + 1) * LANES] for h in range(halves)], axis=0
        ).astype(jnp.bfloat16)
        to_all(rows_out.at[layer], rows_buf.at[layer], 2 + layer)
        rows_buf[layer, me] = rows_out[layer]
        if layer == 0:
            wait_all(info_buf, got.at[1], n - 1)
            facts = info_buf[...].reshape(n * RUN, LANES)
            same = (facts[:, 0:1] == mine[...]).astype(jnp.float32)
            mass = jnp.sum(same * facts[:, LANES // 2 : LANES // 2 + 1], axis=0, keepdims=True)
            share = 1.0 / (1.0 + to_columns(mass)[:, 0:1])
            same = same.reshape(n, RUN, LANES)
            none = jnp.zeros_like(same)
            for h in range(halves):
                full = jnp.concatenate(
                    [same if k == h else none for k in range(halves)], axis=1
                ).reshape(n * RUN * halves, LANES)
                picks.append(jnp.transpose(full).astype(jnp.bfloat16))
        wait_all(rows_buf.at[layer], got.at[2 + layer], n - 1)
        held = rows_buf[layer].reshape(n * RUN * halves, LANES)
        rows = jnp.concatenate(
            [jnp.dot(pick, held, preferred_element_type=jnp.float32) for pick in picks], axis=1
        )
        update = jax.nn.silu(
            jnp.dot(
                (rows * share).astype(jnp.bfloat16), aw[layer], preferred_element_type=jnp.float32
            )
        ).astype(jnp.bfloat16)
        picked = jnp.dot(hot[...], update, preferred_element_type=jnp.float32)
        hidden = hidden + message * picked
    score = jnp.sum(hidden * head[...], axis=1, keepdims=True)
    potential = radius * (1.0 + jnp.tanh(score))
    pot[...] = to_rows(potential)
    last = 2 + layers
    scaled_out[...] = to_rows(weight * potential)
    to_all(scaled_out, scaled_buf, last)
    scaled_buf[me] = scaled_out[...]
    wait_all(scaled_buf, got.at[last], n - 1)
    for k in range(3):
        group = jnp.clip(grid - 1 + k, 0, n_grid - 1)
        near[k * n_atom : (k + 1) * n_atom] = scaled_buf[pl.ds(group * n_atom, n_atom)]
    wait_all(dens_buf, sent.at[0], n_atom - 1)
    wait_all(info_buf, sent.at[1], n - 1)
    for layer in range(layers):
        wait_all(rows_buf.at[layer], sent.at[2 + layer], n - 1)
    wait_all(scaled_buf, sent.at[last], n - 1)


def potential_of(shape, dens, info, mine, hot, hot_t, weights, scale, shift, mw, aw, head):
    n_atom, batches, points = dens.shape
    n = shape[0] * shape[1]
    layers, features, _ = mw.shape
    packed = RUN * (features // LANES)
    return pl.pallas_call(
        functools.partial(potential_kernel, shape, layers),
        out_shape=(
            jax.ShapeDtypeStruct((batches, points), jnp.float32),
            jax.ShapeDtypeStruct((3 * n_atom, batches, points), jnp.float32),
        ),
        in_specs=[VMEM] * 11,
        out_specs=(VMEM, VMEM),
        scratch_shapes=[
            pltpu.VMEM((n_atom, batches, points), jnp.float32),
            pltpu.VMEM((n, RUN, LANES), jnp.float32),
            pltpu.VMEM((layers, packed, LANES), jnp.bfloat16),
            pltpu.VMEM((layers, n, packed, LANES), jnp.bfloat16),
            pltpu.VMEM((batches, points), jnp.float32),
            pltpu.VMEM((n, batches, points), jnp.float32),
            pltpu.SemaphoreType.DMA((3 + layers,)),
            pltpu.SemaphoreType.DMA((3 + layers,)),
        ],
        compiler_params=pltpu.CompilerParams(
            collective_id=0, has_side_effects=True, vmem_limit_bytes=32 << 20
        ),
        cost_estimate=pl.CostEstimate(
            flops=20_000_000_000, bytes_accessed=4_000_000, transcendentals=0
        ),
        name="potential_of",
    )(dens, info, mine, hot, hot_t, weights, scale, shift, mw, aw, head)


def fock_kernel(lists, basis_t, near, low, mid, high, out, scaled):
    step = pl.program_id(0)
    groups, count, depth, points = basis_t.shape
    picks = lists.shape[1]
    width = depth // picks
    owned = out.shape[0] // width

    @pl.when(step == 0)
    def _():
        @pl.loop(0, groups)
        def _(k):
            @pl.loop(0, count)
            def _(b):
                scaled[k, b] = (
                    basis_t[k, b].astype(jnp.float32) * near[pl.ds(k * count + b, 1), :]
                ).astype(jnp.bfloat16)

    out[...] = jnp.zeros_like(out)
    for k, psi in enumerate((low, mid, high)):

        @pl.loop(0, count)
        def _(b, k=k, psi=psi):
            for j in range(picks):
                block = lists[k * count + b, j]

                @pl.when(jnp.logical_and(block >= 0, block < owned))
                def _():
                    at = pl.ds(pl.multiple_of(block * width, width), width)
                    out[at, :] += jnp.dot(
                        scaled[k, b, j * width : (j + 1) * width, :],
                        psi[b],
                        preferred_element_type=jnp.float32,
                    )


def fock_of(lists, basis_t, near, low, mid, high, owned):
    groups, count, depth, points = basis_t.shape
    columns = mid.shape[2]
    wide = min(columns, 512)
    tile = pl.BlockSpec((count, points, wide), lambda i, lists: (0, 0, i))
    return pl.pallas_call(
        fock_kernel,
        out_shape=jax.ShapeDtypeStruct((owned, columns), jnp.float32),
        grid_spec=pltpu.PrefetchScalarGridSpec(
            num_scalar_prefetch=1,
            grid=(columns // wide,),
            in_specs=[
                pl.BlockSpec((groups, count, depth, points), lambda i, lists: (0, 0, 0, 0)),
                pl.BlockSpec((groups * count, points), lambda i, lists: (0, 0)),
                tile,
                tile,
                tile,
            ],
            out_specs=pl.BlockSpec((owned, wide), lambda i, lists: (0, i)),
            scratch_shapes=[pltpu.VMEM((groups, count, depth, points), jnp.bfloat16)],
        ),
        compiler_params=pltpu.CompilerParams(vmem_limit_bytes=60 << 20),
        name="fock_of",
    )(lists, basis_t, near, low, mid, high)


def local(
    basis_values,
    block_lists,
    orbitals,
    point_weights,
    point_atoms,
    embed_scale,
    embed_shift,
    message_weight,
    atom_weight,
    head_weight,
):
    n_grid, n_atom = lax.axis_size("grid"), lax.axis_size("atom")
    own_rows = orbitals.shape[0]
    batches, points, depth = basis_values.shape
    width = depth // block_lists.shape[1]
    owned = own_rows // width
    below = passed_along(orbitals, "grid", 1)
    above = passed_along(orbitals, "grid", -1)
    values = lax.all_gather(basis_values, "atom", axis=0, tiled=True)
    piece_t = jnp.swapaxes(basis_values, 1, 2)
    beside = jnp.stack([passed_along(piece_t, "grid", 1), passed_along(piece_t, "grid", -1)])
    beside = lax.all_gather(beside, "atom", axis=1, tiled=True)
    basis_t = jnp.stack([beside[0], jnp.swapaxes(values, 1, 2), beside[1]])
    first = lax.axis_index("grid") * owned
    lists_low = passed_along(block_lists + 1, "grid", 1) - 1
    lists_high = passed_along(block_lists + 1, "grid", -1) - 1
    lists = jnp.concatenate([lists_low, block_lists, lists_high], axis=0) - first

    total = ATOM_DEV * n_atom
    lead = point_atoms[0]
    shifted = (point_atoms - lead + total // 2) % total - total // 2
    least = jnp.min(shifted)
    start = (lead + least) % total
    place = shifted - least
    lanes = jnp.arange(LANES, dtype=jnp.int32)
    onehot = place[:, None] == lanes[None, :]
    hot = onehot.astype(jnp.bfloat16)
    hot_t = (place[None, :] == lanes[:, None]).astype(jnp.bfloat16)
    mass = jnp.sum(jnp.where(onehot, point_weights[:, None], 0.0), axis=0)[:RUN]
    names = ((start + lanes) % total).astype(jnp.float32)
    mine = jnp.where(lanes < RUN, names, -1.0)[None, :]
    info = jnp.where(lanes[None, :] < LANES // 2, names[:RUN, None], mass[:, None])

    psi, dens = psi_and_density(block_lists - first + owned, values, below, orbitals, above)
    psi_low = passed_along(psi, "grid", 1)
    psi_high = passed_along(psi, "grid", -1)
    potential, near = potential_of(
        (n_grid, n_atom),
        dens.reshape(n_atom, batches, points),
        info,
        mine,
        hot,
        hot_t,
        point_weights.reshape(batches, points),
        embed_scale[None, :],
        embed_shift[None, :],
        message_weight,
        atom_weight,
        head_weight[None, :],
    )
    fock = fock_of(
        lists, basis_t, near.reshape(-1, points), psi_low, psi, psi_high, own_rows
    )
    return (fock, potential.reshape(-1))


def solution(mesh):
    return jax.shard_map(
        local,
        mesh=mesh,
        in_specs=(
            P(("grid", "atom"), None, None),
            P("grid", None),
            P("grid", "atom"),
            P(("grid", "atom")),
            P(("grid", "atom")),
            P(),
            P(),
            P(),
            P(),
            P(),
        ),
        out_specs=(P("grid", "atom"), P(("grid", "atom"))),
        check_vma=False,
    )
```

time: 384 us -> 208 us (0.54)
  the two profiles are of different devices: /device:TPU:4 before, /device:TPU:1 now
where the time goes in v1:
time: 208 us; the launch traced here: 206 us
  Pallas kernels  93.4 us (45%)
  waiting for transfers between devices  57.4 us (28%)
  starting transfers between devices  21.6 us (10%)
  between operations  15.6 us (8%)
  local copies, waits for them, and re-layouts  9.73 us (5%)
  other arithmetic  8.5 us (4%)
    pallas_call x1, Pallas kernels, potential_of(): pl.pallas_call(functools.partial(potential_kernel, shape, layers), out_sh...  60.8 us
    ppermute x8, waiting for transfers between devices, passed_along(): lax.ppermute(value, axis, [(source, source + steps) for source in range(l...  57.3 us
    pallas_call x1, Pallas kernels, fock_of(): pl.pallas_call(fock_kernel, out_shape=jax.ShapeDtypeStruct((owned, column...  22.8 us
    ppermute x8, starting transfers between devices, passed_along(): lax.ppermute(value, axis, [(source, source + steps) for source in range(l...  21.5 us
    pallas_call x1, Pallas kernels, psi_and_density(): pl.pallas_call(psi_kernel, out_shape=(jax.ShapeDtypeStruct((count, points...  9.9 us
    unnamed x23, local copies, waits for them, and re-layouts  4.31 us
  transfers between devices with their start and end apart: 10, of which 2 were waited for; matrix products, arithmetic and copies ran while one was open for 8% of the time, Pallas kernels for 34%

profile of v1, /device:TPU:1, one launch (start us, length us, event | category | flops | bytes accessed | tf_op | source)
XLA Modules:
  0.0 206.3 jit_solution(3187062554560004238)
XLA Ops:
  7.2 4.5 %collective-permute-start.4 = (bf16[1536,1024]{1,0:T(8,128)(2,1)}, bf16[1536,1024]{1,0:T(8,128)(2,1)}, u32[]{:S(2)}, u32[]{:S(2)}) collective-permute-start(bf16[1536,1024]{1,0:T(8,128)(2,1)} %own.1), channel_id=1, source_target_pairs={{0,4},{4,8},{8,12},{12,16},{16,20},{20,24},{24,28},{1,5},{5,9},{9,... | collective-permute-start | bytes 9437192 | tf_op jit(solution)/shard_map/ppermute | solution.py:19
  11.7 1.9 collective-permute-start.5
  13.7 1.1 copy.24
  14.9 1.9 collective-permute-start.3
  16.8 3.6 %collective-permute-start.2 = (bf16[2,512,128]{2,1,0:T(8,128)(2,1)S(1)}, bf16[2,512,128]{2,1,0:T(8,128)(2,1)S(1)}, u32[]{:S(2)}, u32[]{:S(2)}) collective-permute-start(bf16[2,512,128]{2,1,0:T(8,128)(2,1)S(1)} %bitcast.25), channel_id=1, source_target_pairs={{0,4},{4,8},{8,12},{12,16},{16,20},{20,24},{24,28},{1,5},{5,9},{9,... | collective-permute-start | bytes 786440 | tf_op jit(solution)/shard_map/ppermute | solution.py:19
  20.4 0.7 broadcast_add_fusion.2
  21.1 1.9 collective-permute-start.1
  23.0 1.2 slice.17
  24.2 2.0 fusion.8
  27.5 0.8 copy.26
  28.3 0.6 broadcast_subtract_fusion.1
  28.9 0.8 select_reduce_fusion
  29.8 0.1 fusion.hot
  29.9 57.2 %collective-permute-done.3 = bf16[2,512,128]{2,1,0:T(8,128)(2,1)S(1)} collective-permute-done((bf16[2,512,128]{2,1,0:T(8,128)(2,1)S(1)}, bf16[2,512,128]{2,1,0:T(8,128)(2,1)S(1)}, u32[]{:S(2)}, u32[]{:S(2)}) %collective-permute-start.3) | collective-permute-done | bytes 262176 | tf_op jit(solution)/shard_map/ppermute | solution.py:19
  87.1 1.9 collective-permute-start
  89.0 0.8 pad_maximum_fusion.1
  89.9 0.1 broadcast_select_fusion.info
  90.0 0.1 collective-permute-done
  90.1 0.8 pad_add_fusion
  90.9 0.1 copy.22
  91.0 0.6 broadcast_subtract_fusion.lists
  91.6 2.3 %copy.25 = bf16[8,128,512]{1,2,0:T(8,128)(2,1)} copy(bf16[8,128,512]{2,1,0:T(8,128)(2,1)} %all-gather.5.cloned.1.call-done.basis) | data formatting | bytes 2097152 | tf_op jit(solution)/shard_map/all_gather | solution.py:345
  94.0 1.2 copy-done
  95.2 9.9 %psi_and_density.1 = (bf16[8,128,1024]{2,1,0:T(8,128)(2,1)S(1)}, f32[8,128]{1,0:T(8,128)S(1)}) custom-call(s32[8,4]{1,0:T(8,128)S(1)} %subtract_add_fusion.lists, bf16[8,128,512]{2,1,0:T(8,128)(2,1)S(1)} %copy-done, bf16[1536,1024]{1,0:T(8,128)(2,1)} %collective-permute-done.4.below, bf16[1536,1024]{1,0:T(8,128)(2,1)} %own.1, ...), custom_call_target="tpu_custom_call" | custom-call | flops 1073741824 | bytes 12582912 | tf_op jit(solution)/shard_map/psi_and_density/pallas_call | solution.py:82
  105.1 2.3 %collective-permute-start.7 = (bf16[8,128,1024]{2,1,0:T(8,128)(2,1)S(1)}, bf16[8,128,1024]{2,1,0:T(8,128)(2,1)}, u32[]{:S(2)}, u32[]{:S(2)}) collective-permute-start(bf16[8,128,1024]{2,1,0:T(8,128)(2,1)S(1)} %get-tuple-element.8.mid), channel_id=1, source_target_pairs={{4,0},{8,4},{12,8},{16,12},{20,16},{24,20},{28,24},{5,1},{9,5},{13... | collective-permute-start | bytes 6291464 | tf_op jit(solution)/shard_map/ppermute | solution.py:19
  107.4 3.4 %collective-permute-start.6 = (bf16[8,128,1024]{2,1,0:T(8,128)(2,1)S(1)}, bf16[8,128,1024]{2,1,0:T(8,128)(2,1)}, u32[]{:S(2)}, u32[]{:S(2)}) collective-permute-start(bf16[8,128,1024]{2,1,0:T(8,128)(2,1)S(1)} %get-tuple-element.8.mid), channel_id=1, source_target_pairs={{0,4},{4,8},{8,12},{12,16},{16,20},{20,24},{24,28},{1,5},{5,9},{9,... | collective-permute-start | bytes 6291464 | tf_op jit(solution)/shard_map/ppermute | solution.py:19
  110.9 60.8 %potential_of.1 = (f32[2,128]{1,0:T(2,128)S(1)}, f32[12,2,128]{2,1,0:T(2,128)S(1)}) custom-call(f32[4,2,128]{2,1,0:T(2,128)S(1)} %bitcast.19, f32[8,128]{1,0:T(8,128)S(1)} %broadcast_select_fusion.info, f32[1,128]{1,0:T(1,128)S(1)} %compare_select_fusion.6.mine, bf16[256,128]{1,0:T(8,128)(2,1)S(1)} %fusion.hot, bf16[128,256]{1,0:T(8,128)(2,1)S(1)} %fusion.1.hot_t, ...), custom_call_target="tpu_custom_call" | custom-call | flops 20000000000 | bytes 4000000 | tf_op jit(solution)/shard_map/potential_of/pallas_call | solution.py:237
  171.7 0.6 copy-done.2
  172.3 1.8 fusion.10
  174.1 2.0 pad_maximum_fusion.basis_t
  176.1 22.8 %fock_of.1 = f32[1536,1024]{1,0:T(8,128)} custom-call(s32[24,4]{1,0:T(8,128)} %broadcast_subtract_fusion.lists, bf16[3,8,512,128]{3,2,1,0:T(8,128)(2,1)} %pad_maximum_fusion.basis_t, f32[24,128]{1,0:T(8,128)} %bitcast.16, bf16[8,128,1024]{2,1,0:T(8,128)(2,1)} %collective-permute-done.6.low, bf16[8,128,1024]{2,1,0:T(8,128)(2,1)} %copy-done.1, ...), custom_call_target="tpu_custom_call" | custom-call | tf_op jit(solution)/shard_map/fock_of/pallas_call | solution.py:305
  198.9 0.6 copy.28
  (37 shorter events, 0.3 us)
Async XLA Ops:
  7.2 84.4 %all-gather.5.cloned.1.call-start = ((), (), s32[]{:S(2)}) async-start(), calls=%async_computation.1 | async-start | bytes 1310720 | tf_op jit(solution)/shard_map/all_gather | solution.py:345
  7.2 86.8 %collective-permute-start.4 = (bf16[1536,1024]{1,0:T(8,128)(2,1)}, bf16[1536,1024]{1,0:T(8,128)(2,1)}, u32[]{:S(2)}, u32[]{:S(2)}) collective-permute-start(bf16[1536,1024]{1,0:T(8,128)(2,1)} %own.1), channel_id=1, source_target_pairs={{0,4},{4,8},{8,12},{12,16},{16,20},{20,24},{24,28},{1,5},{5,9},{9,... | collective-permute-start | bytes 9437192 | tf_op jit(solution)/shard_map/ppermute | solution.py:19
  11.7 82.2 %collective-permute-start.5 = (bf16[1536,1024]{1,0:T(8,128)(2,1)}, bf16[1536,1024]{1,0:T(8,128)(2,1)}, u32[]{:S(2)}, u32[]{:S(2)}) collective-permute-start(bf16[1536,1024]{1,0:T(8,128)(2,1)} %own.1), channel_id=1, source_target_pairs={{4,0},{8,4},{12,8},{16,12},{20,16},{24,20},{28,24},{5,1},{9,5},{13... | collective-permute-start | bytes 9437192 | tf_op jit(solution)/shard_map/ppermute | solution.py:19
  13.7 158.6 %all-gather.3.cloned.1.call-start = ((), (), s32[]{:S(2)}) async-start(), calls=%async_computation | async-start | bytes 2621440 | tf_op jit(solution)/shard_map/all_gather | solution.py:348
  14.9 72.2 %collective-permute-start.3 = (bf16[2,512,128]{2,1,0:T(8,128)(2,1)S(1)}, bf16[2,512,128]{2,1,0:T(8,128)(2,1)S(1)}, u32[]{:S(2)}, u32[]{:S(2)}) collective-permute-start(bf16[2,512,128]{2,1,0:T(8,128)(2,1)S(1)} %bitcast.24), channel_id=1, source_target_pairs={{4,0},{8,4},{12,8},{16,12},{20,16},{24,20},{28,24},{5,1},{9,5},{13... | collective-permute-start | bytes 786440 | tf_op jit(solution)/shard_map/ppermute | solution.py:19
  16.8 72.2 %collective-permute-start.2 = (bf16[2,512,128]{2,1,0:T(8,128)(2,1)S(1)}, bf16[2,512,128]{2,1,0:T(8,128)(2,1)S(1)}, u32[]{:S(2)}, u32[]{:S(2)}) collective-permute-start(bf16[2,512,128]{2,1,0:T(8,128)(2,1)S(1)} %bitcast.25), channel_id=1, source_target_pairs={{0,4},{4,8},{8,12},{12,16},{16,20},{20,24},{24,28},{1,5},{5,9},{9,... | collective-permute-start | bytes 786440 | tf_op jit(solution)/shard_map/ppermute | solution.py:19
  21.1 68.9 %collective-permute-start.1 = (s32[8,4]{0,1:T(4,128)S(1)}, s32[8,4]{0,1:T(4,128)S(1)}, u32[]{:S(2)}, u32[]{:S(2)}) collective-permute-start(s32[8,4]{0,1:T(4,128)S(1)} %broadcast_add_fusion.2), channel_id=1, source_target_pairs={{4,0},{8,4},{12,8},{16,12},{20,16},{24,20},{28,24},{5,1},{9,5},{13... | collective-permute-start | bytes 392 | tf_op jit(solution)/shard_map/ppermute | solution.py:19
  87.1 3.0 %collective-permute-start = (s32[8,4]{0,1:T(4,128)S(1)}, s32[8,4]{0,1:T(4,128)S(1)}, u32[]{:S(2)}, u32[]{:S(2)}) collective-permute-start(s32[8,4]{0,1:T(4,128)S(1)} %broadcast_add_fusion.2), channel_id=1, source_target_pairs={{0,4},{4,8},{8,12},{12,16},{16,20},{20,24},{24,28},{1,5},{5,9},{9,... | collective-permute-start | bytes 392 | tf_op jit(solution)/shard_map/ppermute | solution.py:19
  91.6 19.3 %copy-start.3 = (f32[256]{0:T(256)S(1)}, f32[256]{0:T(256)}, u32[]{:S(2)}) copy-start(f32[256]{0:T(256)} %param.13) | copy-start | bytes 3076
  91.6 19.3 %copy-start.4 = (bf16[2,256,256]{2,1,0:T(8,128)(2,1)S(1)}, bf16[2,256,256]{2,1,0:T(8,128)(2,1)}, u32[]{:S(2)}) copy-start(bf16[2,256,256]{2,1,0:T(8,128)(2,1)} %mw.1) | copy-start | bytes 786436
  91.6 19.3 %copy-start.5 = (bf16[2,256,256]{2,1,0:T(8,128)(2,1)S(1)}, bf16[2,256,256]{2,1,0:T(8,128)(2,1)}, u32[]{:S(2)}) copy-start(bf16[2,256,256]{2,1,0:T(8,128)(2,1)} %aw.1) | copy-start | bytes 786436
  91.6 19.3 %copy-start.6 = (f32[256]{0:T(256)S(1)}, f32[256]{0:T(256)}, u32[]{:S(2)}) copy-start(f32[256]{0:T(256)} %param.15) | copy-start | bytes 3076
  91.6 19.3 %copy-start.7 = (f32[256]{0:T(256)S(1)}, f32[256]{0:T(256)}, u32[]{:S(2)}) copy-start(f32[256]{0:T(256)} %param.16) | copy-start | bytes 3076
  91.6 19.3 %copy-start.8 = (f32[256]{0:T(256)S(1)}, f32[256]{0:T(256)}, u32[]{:S(2)}) copy-start(f32[256]{0:T(256)} %param.19) | copy-start | bytes 3076
  94.0 1.2 copy-start
  105.1 66.6 %copy-start.1 = (bf16[8,128,1024]{2,1,0:T(8,128)(2,1)}, bf16[8,128,1024]{2,1,0:T(8,128)(2,1)S(1)}, u32[]{:S(2)}) copy-start(bf16[8,128,1024]{2,1,0:T(8,128)(2,1)S(1)} %get-tuple-element.8.mid) | copy-start | bytes 6291460
  105.1 71.0 %collective-permute-start.7 = (bf16[8,128,1024]{2,1,0:T(8,128)(2,1)S(1)}, bf16[8,128,1024]{2,1,0:T(8,128)(2,1)}, u32[]{:S(2)}, u32[]{:S(2)}) collective-permute-start(bf16[8,128,1024]{2,1,0:T(8,128)(2,1)S(1)} %get-tuple-element.8.mid), channel_id=1, source_target_pairs={{4,0},{8,4},{12,8},{16,12},{20,16},{24,20},{28,24},{5,1},{9,5},{13... | collective-permute-start | bytes 6291464 | tf_op jit(solution)/shard_map/ppermute | solution.py:19
  107.4 68.7 %collective-permute-start.6 = (bf16[8,128,1024]{2,1,0:T(8,128)(2,1)S(1)}, bf16[8,128,1024]{2,1,0:T(8,128)(2,1)}, u32[]{:S(2)}, u32[]{:S(2)}) collective-permute-start(bf16[8,128,1024]{2,1,0:T(8,128)(2,1)S(1)} %get-tuple-element.8.mid), channel_id=1, source_target_pairs={{0,4},{4,8},{8,12},{12,16},{16,20},{20,24},{24,28},{1,5},{5,9},{9,... | collective-permute-start | bytes 6291464 | tf_op jit(solution)/shard_map/ppermute | solution.py:19
  171.7 0.6 copy-start.2
  172.3 1.9 copy-start.9
Sparse Core Ops, SparseCore 0:
  13.8 28.8 all-gather.4
  90.0 51.3 all-gather.2

commit v2 on v1

--- a/solution.py
+++ b/solution.py
@@ -13,10 +13,209 @@
 MESH = pl.DeviceIdType.MESH
 
 
-def passed_along(value, axis, steps):
-    count = lax.axis_size(axis)
-    leading, last = (max(0, -steps), min(count, count - steps))
-    return lax.ppermute(value, axis, [(source, source + steps) for source in range(leading, last)])
+def wait_bytes(ref, sem):
+    pltpu.make_async_copy(ref, ref, sem).wait()
+
+
+class Halo:
+    def __init__(self, n_grid, rounds, source, low, high, relay, sent, got, passed):
+        self.n_grid, self.rounds, self.middle = n_grid, rounds, n_grid // 2
+        self.source, self.low, self.high, self.relay = source, low, high, relay
+        self.sent, self.got, self.passed = sent, got, passed
+        self.size = source.shape[0] // (2 * rounds)
+        self.grid, self.atom = lax.axis_index("grid"), lax.axis_index("atom")
+
+    def copy(self, source, target, sent, got, grid):
+        pltpu.make_async_remote_copy(
+            src_ref=source,
+            dst_ref=target,
+            send_sem=sent,
+            recv_sem=got,
+            device_id=(grid, self.atom),
+            device_id_type=MESH,
+        ).start()
+
+    def send(self, r):
+        grid, last, size = self.grid, self.n_grid - 1, self.size
+        for way, (step, held, split, able) in enumerate(
+            (
+                (1, self.low, self.middle - 1, grid < last),
+                (-1, self.high, self.middle, grid > 0),
+            )
+        ):
+            for side, end in enumerate((0, last)):
+                part = pl.ds((side * self.rounds + r) * size, size)
+
+                @pl.when(jnp.logical_and(able, grid != split))
+                def _():
+                    self.copy(
+                        self.source.at[part], held.at[part],
+                        self.sent.at[way], self.got.at[way], grid + step,
+                    )
+
+                @pl.when(grid == split)
+                def _():
+                    self.copy(
+                        self.source.at[part], self.relay.at[way, pl.ds(r * size, size)],
+                        self.sent.at[way], self.passed.at[way, r], end,
+                    )
+
+    def forward(self, r):
+        size = self.size
+        for side, end in enumerate((0, self.n_grid - 1)):
+
+            @pl.when(self.grid == end)
+            def _():
+                for way, (held, to) in enumerate(
+                    ((self.low, self.middle), (self.high, self.middle - 1))
+                ):
+                    piece = self.relay.at[way, pl.ds(r * size, size)]
+                    wait_bytes(piece, self.passed.at[way, r])
+                    part = pl.ds((side * self.rounds + r) * size, size)
+                    self.copy(piece, held.at[part], self.sent.at[2 + way], self.got.at[way], to)
+
+    def finish(self):
+        grid, last = self.grid, self.n_grid - 1
+
+        @pl.when(grid > 0)
+        def _():
+            wait_bytes(self.low, self.got.at[0])
+            wait_bytes(self.source, self.sent.at[1])
+
+        @pl.when(grid < last)
+        def _():
+            wait_bytes(self.high, self.got.at[1])
+            wait_bytes(self.source, self.sent.at[0])
+
+        @pl.when(jnp.logical_or(grid == 0, grid == last))
+        def _():
+            for way in range(2):
+                wait_bytes(self.relay.at[way], self.sent.at[2 + way])
+
+
+def halo_scratch(rounds):
+    return [
+        pltpu.SemaphoreType.DMA((4,)),
+        pltpu.SemaphoreType.DMA((2,)),
+        pltpu.SemaphoreType.DMA((2, rounds)),
+    ]
+
+
+def meet_all(shape):
+    n_grid, n_atom = shape
+    n = n_grid * n_atom
+    me = lax.axis_index("grid") * n_atom + lax.axis_index("atom")
+    barrier = pltpu.get_barrier_semaphore()
+
+    @pl.loop(1, n)
+    def _(d):
+        t = lax.rem(me + d, n)
+        pl.semaphore_signal(
+            barrier, inc=1, device_id=(t // n_atom, lax.rem(t, n_atom)), device_id_type=MESH
+        )
+
+    pl.semaphore_wait(barrier, n - 1)
+
+
+ROUNDS = 4
+
+
+def halo_kernel(
+    shape, own, piece, names, low, high, basis, all_names, relay,
+    sent, got, passed, piece_sent, piece_got, name_sent, name_got,
+):
+    n_grid, n_atom = shape
+    grid, atom = lax.axis_index("grid"), lax.axis_index("atom")
+    meet_all(shape)
+    halo = Halo(n_grid, ROUNDS, own, low, high, relay, sent, got, passed)
+
+    def send(source, target, sent_sem, got_sem, to):
+        pltpu.make_async_remote_copy(
+            src_ref=source,
+            dst_ref=target,
+            send_sem=sent_sem,
+            recv_sem=got_sem,
+            device_id=to,
+            device_id_type=MESH,
+        ).start()
+
+    sides = ((0, 1, grid < n_grid - 1, grid > 0), (2, -1, grid > 0, grid < n_grid - 1))
+    for slot, step, able, _ in sides:
+
+        @pl.when(able)
+        def _():
+            send(names, all_names.at[slot], name_sent.at[slot], name_got.at[slot], (grid + step, atom))
+            send(piece, basis.at[slot, atom], piece_sent.at[slot], piece_got.at[slot], (grid + step, atom))
+
+    def to_peers(source, slot, k):
+        @pl.loop(1, n_atom)
+        def _(d):
+            to = lax.rem(atom + d, n_atom)
+            send(source, basis.at[slot, atom], piece_sent.at[k], piece_got.at[k], (grid, to))
+
+    to_peers(piece, 1, 1)
+    for r in range(ROUNDS):
+        halo.send(r)
+    basis[1, atom] = piece[...]
+    all_names[1] = names[...]
+    for slot, _, _, filled in sides:
+
+        @pl.when(filled)
+        def _():
+            wait_bytes(piece, piece_got.at[slot])
+            to_peers(basis.at[slot, atom], slot, 3 + slot // 2)
+
+        @pl.when(jnp.logical_not(filled))
+        def _():
+            all_names[slot] = jnp.full_like(names, -1)
+
+    for r in range(ROUNDS):
+        halo.forward(r)
+    peers = pl.ds(0, n_atom - 1)
+    wait_bytes(basis.at[1, peers], piece_got.at[1])
+    wait_bytes(basis.at[1, peers], piece_sent.at[1])
+    for slot, _, able, filled in sides:
+
+        @pl.when(able)
+        def _():
+            wait_bytes(piece, piece_sent.at[slot])
+            wait_bytes(names, name_sent.at[slot])
+
+        @pl.when(filled)
+        def _():
+            wait_bytes(names, name_got.at[slot])
+            wait_bytes(basis.at[slot, peers], piece_got.at[3 + slot // 2])
+            wait_bytes(basis.at[slot, peers], piece_sent.at[3 + slot // 2])
+
+    halo.finish()
+
+
+def halo_of(shape, own, piece, names):
+    rows, columns = own.shape
+    anywhere = pl.BlockSpec(memory_space=pl.ANY)
+    return pl.pallas_call(
+        functools.partial(halo_kernel, shape),
+        out_shape=(
+            jax.ShapeDtypeStruct(own.shape, own.dtype),
+            jax.ShapeDtypeStruct(own.shape, own.dtype),
+            jax.ShapeDtypeStruct((3, shape[1], *piece.shape), piece.dtype),
+            jax.ShapeDtypeStruct((3, *names.shape), names.dtype),
+            jax.ShapeDtypeStruct((2, rows // 2, columns), own.dtype),
+        ),
+        in_specs=[anywhere, VMEM, VMEM],
+        out_specs=(anywhere, anywhere, VMEM, VMEM, anywhere),
+        scratch_shapes=halo_scratch(ROUNDS)
+        + [
+            pltpu.SemaphoreType.DMA((5,)),
+            pltpu.SemaphoreType.DMA((5,)),
+            pltpu.SemaphoreType.DMA((3,)),
+            pltpu.SemaphoreType.DMA((3,)),
+        ],
+        compiler_params=pltpu.CompilerParams(
+            collective_id=1, has_side_effects=True, vmem_limit_bytes=40 << 20
+        ),
+        name="halo_of",
+    )(own, piece, names)
 
 
 def to_columns(rows):
@@ -35,7 +234,7 @@
     return jnp.concatenate(parts, axis=0)
 
 
-def psi_kernel(lists, basis, below, own, above, psi, dens, rows, sums):
+def psi_kernel(lists, basis_t, below, own, above, psi, dens, rows, sums, basis):
     step = pl.program_id(0)
     owned = own.shape[0]
     rows[0:owned, :] = below[...]
@@ -49,6 +248,8 @@
     @pl.when(step == 0)
     def _():
         sums[...] = jnp.zeros_like(sums)
+        for b in range(count):
+            basis[b] = jnp.transpose(basis_t[0, b])
 
     @pl.loop(0, count)
     def _(b):
@@ -74,9 +275,9 @@
             dens[b : b + 1, :] = jnp.sum(jnp.transpose(sums[b]), axis=0, keepdims=True)
 
 
-def psi_and_density(lists, basis, below, own, above):
+def psi_and_density(lists, basis_t, below, own, above):
     owned, columns = own.shape
-    count, points, depth = basis.shape
+    _, count, depth, points = basis_t.shape
     wide = min(columns, 256)
     tile = pl.BlockSpec((owned, wide), lambda i, lists: (0, i))
     return pl.pallas_call(
@@ -89,7 +290,7 @@
             num_scalar_prefetch=1,
             grid=(columns // wide,),
             in_specs=[
-                pl.BlockSpec((count, points, depth), lambda i, lists: (0, 0, 0)),
+                pl.BlockSpec((1, count, depth, points), lambda i, lists: (1, 0, 0, 0)),
                 tile,
                 tile,
                 tile,
@@ -101,6 +302,7 @@
             scratch_shapes=[
                 pltpu.VMEM((3 * owned, wide), jnp.bfloat16),
                 pltpu.VMEM((count, points, LANES), jnp.float32),
+                pltpu.VMEM((count, points, depth), jnp.bfloat16),
             ],
         ),
         compiler_params=pltpu.CompilerParams(vmem_limit_bytes=48 << 20),
@@ -110,12 +312,14 @@
             transcendentals=0,
         ),
         name="psi_and_density",
-    )(lists, basis, below, own, above)
+    )(lists, basis_t, below, own, above)
 
 
 def potential_kernel(
-    shape, layers, dens, info, mine, hot, hot_t, weights, scale, shift, mw, aw, head,
-    pot, near, dens_buf, info_buf, rows_out, rows_buf, scaled_out, scaled_buf, sent, got,
+    shape, layers, psi, dens, info, mine, hot, hot_t, weights, scale, shift, mw, aw, head,
+    pot, near, psi_low, psi_high, relay,
+    dens_buf, info_buf, rows_out, rows_buf, scaled_out, scaled_buf, sent, got,
+    psi_sent, psi_got, psi_passed,
 ):
     n_grid, n_atom = shape
     n = n_grid * n_atom
@@ -142,13 +346,8 @@
         part = held.at[pl.ds(0, count)]
         pltpu.make_async_copy(part, part, sem).wait()
 
-    barrier = pltpu.get_barrier_semaphore()
-
-    @pl.loop(1, n)
-    def _(d):
-        pl.semaphore_signal(barrier, inc=1, device_id=other(d), device_id_type=MESH)
-
-    pl.semaphore_wait(barrier, n - 1)
+    meet_all(shape)
+    halo = Halo(n_grid, layers + 2, psi, psi_low, psi_high, relay, psi_sent, psi_got, psi_passed)
 
     @pl.loop(1, n_atom)
     def _(d):
@@ -163,6 +362,7 @@
         ).start()
 
     to_all(info, info_buf, 1)
+    halo.send(0)
     dens_buf[atom] = dens[atom]
     info_buf[me] = info[...]
     weight = to_columns(weights[...])[:, 0:1]
@@ -185,6 +385,7 @@
             [part[0:RUN, h * LANES : (h + 1) * LANES] for h in range(halves)], axis=0
         ).astype(jnp.bfloat16)
         to_all(rows_out.at[layer], rows_buf.at[layer], 2 + layer)
+        halo.send(1 + layer)
         rows_buf[layer, me] = rows_out[layer]
         if layer == 0:
             wait_all(info_buf, got.at[1], n - 1)
@@ -200,6 +401,7 @@
                 ).reshape(n * RUN * halves, LANES)
                 picks.append(jnp.transpose(full).astype(jnp.bfloat16))
         wait_all(rows_buf.at[layer], got.at[2 + layer], n - 1)
+        halo.forward(layer)
         held = rows_buf[layer].reshape(n * RUN * halves, LANES)
         rows = jnp.concatenate(
             [jnp.dot(pick, held, preferred_element_type=jnp.float32) for pick in picks], axis=1
@@ -217,8 +419,11 @@
     last = 2 + layers
     scaled_out[...] = to_rows(weight * potential)
     to_all(scaled_out, scaled_buf, last)
+    halo.send(layers + 1)
     scaled_buf[me] = scaled_out[...]
     wait_all(scaled_buf, got.at[last], n - 1)
+    halo.forward(layers)
+    halo.forward(layers + 1)
     for k in range(3):
         group = jnp.clip(grid - 1 + k, 0, n_grid - 1)
         near[k * n_atom : (k + 1) * n_atom] = scaled_buf[pl.ds(group * n_atom, n_atom)]
@@ -227,21 +432,26 @@
     for layer in range(layers):
         wait_all(rows_buf.at[layer], sent.at[2 + layer], n - 1)
     wait_all(scaled_buf, sent.at[last], n - 1)
-
-
-def potential_of(shape, dens, info, mine, hot, hot_t, weights, scale, shift, mw, aw, head):
+    halo.finish()
+
+
+def potential_of(shape, psi, dens, info, mine, hot, hot_t, weights, scale, shift, mw, aw, head):
     n_atom, batches, points = dens.shape
     n = shape[0] * shape[1]
     layers, features, _ = mw.shape
     packed = RUN * (features // LANES)
+    anywhere = pl.BlockSpec(memory_space=pl.ANY)
     return pl.pallas_call(
         functools.partial(potential_kernel, shape, layers),
         out_shape=(
             jax.ShapeDtypeStruct((batches, points), jnp.float32),
             jax.ShapeDtypeStruct((3 * n_atom, batches, points), jnp.float32),
-        ),
-        in_specs=[VMEM] * 11,
-        out_specs=(VMEM, VMEM),
+            jax.ShapeDtypeStruct(psi.shape, psi.dtype),
+            jax.ShapeDtypeStruct(psi.shape, psi.dtype),
+            jax.ShapeDtypeStruct((2, psi.shape[0] // 2, *psi.shape[1:]), psi.dtype),
+        ),
+        in_specs=[anywhere] + [VMEM] * 11,
+        out_specs=(VMEM, VMEM, anywhere, anywhere, anywhere),
         scratch_shapes=[
             pltpu.VMEM((n_atom, batches, points), jnp.float32),
             pltpu.VMEM((n, RUN, LANES), jnp.float32),
@@ -251,7 +461,8 @@
             pltpu.VMEM((n, batches, points), jnp.float32),
             pltpu.SemaphoreType.DMA((3 + layers,)),
             pltpu.SemaphoreType.DMA((3 + layers,)),
-        ],
+        ]
+        + halo_scratch(layers + 2),
         compiler_params=pltpu.CompilerParams(
             collective_id=0, has_side_effects=True, vmem_limit_bytes=32 << 20
         ),
@@ -259,7 +470,7 @@
             flops=20_000_000_000, bytes_accessed=4_000_000, transcendentals=0
         ),
         name="potential_of",
-    )(dens, info, mine, hot, hot_t, weights, scale, shift, mw, aw, head)
+    )(psi, dens, info, mine, hot, hot_t, weights, scale, shift, mw, aw, head)
 
 
 def fock_kernel(lists, basis_t, near, low, mid, high, out, scaled):
@@ -340,17 +551,14 @@
     batches, points, depth = basis_values.shape
     width = depth // block_lists.shape[1]
     owned = own_rows // width
-    below = passed_along(orbitals, "grid", 1)
-    above = passed_along(orbitals, "grid", -1)
-    values = lax.all_gather(basis_values, "atom", axis=0, tiled=True)
-    piece_t = jnp.swapaxes(basis_values, 1, 2)
-    beside = jnp.stack([passed_along(piece_t, "grid", 1), passed_along(piece_t, "grid", -1)])
-    beside = lax.all_gather(beside, "atom", axis=1, tiled=True)
-    basis_t = jnp.stack([beside[0], jnp.swapaxes(values, 1, 2), beside[1]])
+    shape = (n_grid, n_atom)
     first = lax.axis_index("grid") * owned
-    lists_low = passed_along(block_lists + 1, "grid", 1) - 1
-    lists_high = passed_along(block_lists + 1, "grid", -1) - 1
-    lists = jnp.concatenate([lists_low, block_lists, lists_high], axis=0) - first
+    names = jnp.pad(block_lists, ((0, 0), (0, LANES - block_lists.shape[1])))
+    below, above, basis_t, names, _ = halo_of(
+        shape, orbitals, jnp.swapaxes(basis_values, 1, 2), names
+    )
+    basis_t = basis_t.reshape(3, n_atom * batches, depth, points)
+    lists = names[:, :, : block_lists.shape[1]].reshape(-1, block_lists.shape[1]) - first
 
     total = ATOM_DEV * n_atom
     lead = point_atoms[0]
@@ -367,11 +575,10 @@
     mine = jnp.where(lanes < RUN, names, -1.0)[None, :]
     info = jnp.where(lanes[None, :] < LANES // 2, names[:RUN, None], mass[:, None])
 
-    psi, dens = psi_and_density(block_lists - first + owned, values, below, orbitals, above)
-    psi_low = passed_along(psi, "grid", 1)
-    psi_high = passed_along(psi, "grid", -1)
-    potential, near = potential_of(
-        (n_grid, n_atom),
+    psi, dens = psi_and_density(block_lists - first + owned, basis_t, below, orbitals, above)
+    potential, near, psi_low, psi_high, _ = potential_of(
+        shape,
+        psi,
         dens.reshape(n_atom, batches, points),
         info,
         mine,

time: 208 us -> 169 us (0.81)
  the two profiles are of different devices: /device:TPU:1 before, /device:TPU:4 now
where the time goes in v2:
time: 169 us; the launch traced here: 168 us
  Pallas kernels  152 us (90%)
  local copies, waits for them, and re-layouts  10.3 us (6%)
  other arithmetic  4.31 us (3%)
  between operations  2.13 us (1%)
    pallas_call x1, Pallas kernels, halo_of(): pl.pallas_call(functools.partial(halo_kernel, shape), out_shape=(jax.Shap...  68.9 us
    pallas_call x1, Pallas kernels, potential_of(): pl.pallas_call(functools.partial(potential_kernel, shape, layers), out_sh...  52.5 us
    pallas_call x1, Pallas kernels, fock_of(): pl.pallas_call(fock_kernel, out_shape=jax.ShapeDtypeStruct((owned, column...  20.1 us
    pallas_call x1, Pallas kernels, psi_and_density(): pl.pallas_call(psi_kernel, out_shape=(jax.ShapeDtypeStruct((count, points...  10.1 us
    unnamed x29, local copies, waits for them, and re-layouts  9.14 us

profile of v2, /device:TPU:4, one launch (start us, length us, event | category | flops | bytes accessed | tf_op | source)
XLA Modules:
  0.0 168.4 jit_solution(3316519535227028458)
XLA Ops:
  0.6 1.2 slice.13
  1.8 2.0 %fusion.8 = (s32[]{:T(128)}, s32[256]{0:T(256)S(1)}) fusion(s32[256]{0:T(256)} %param.14, s32[]{:T(128)} %bitcast.4), kind=kLoop, calls=%fused_computation.26 | loop fusion | flops 3839 | bytes 2056 | tf_op jit(solution)/shard_map/reduce_min | solution.py:566
  5.1 0.7 broadcast_subtract_fusion
  5.8 0.8 select_reduce_fusion
  6.6 0.1 broadcast_select_fusion.info
  6.7 0.8 copy.18
  7.5 0.1 fusion.hot
  7.6 1.1 copy.17
  8.7 68.9 %halo_of.1 = (bf16[1536,1024]{1,0:T(8,128)(2,1)S(1)}, bf16[1536,1024]{1,0:T(8,128)(2,1)S(1)}, bf16[3,4,2,512,128]{4,3,2,1,0:T(8,128)(2,1)S(1)}, s32[3,8,128]{2,1,0:T(8,128)S(1)}, bf16[2,768,1024]{2,1,0:T(8,128)(2,1)}) custom-call(bf16[1536,1024]{1,0:T(8,128)(2,1)} %own.3, bf16[2,512,128]{2,1,0:T(8,128)(2,1)S(1)} %bitcast.16, s32[8,128]{1,0:T(8,128)S(1)} %pad.4.names), custom_call_target="tpu_custom_call" | custom-call | tf_op jit(solution)/shard_map/halo_of/pallas_call | solution.py:196
  77.7 0.0 copy-start.1
  77.7 1.7 copy-done.1
  79.3 1.7 copy-done.2
  81.0 0.6 subtract_bitcast_fusion.lists
  81.7 0.0 copy-start.11
  81.7 0.0 copy-start.12
  81.7 10.1 %psi_and_density.1 = (bf16[8,128,1024]{2,1,0:T(8,128)(2,1)S(1)}, f32[8,128]{1,0:T(8,128)S(1)}) custom-call(s32[8,4]{1,0:T(8,128)S(1)} %subtract_add_fusion.lists, bf16[3,8,512,128]{3,2,1,0:T(8,128)(2,1)S(1)} %bitcast.14, bf16[1536,1024]{1,0:T(8,128)(2,1)} %copy-done.1, bf16[1536,1024]{1,0:T(8,128)(2,1)} %own.3, bf16[1536,1024]{1,0:T(8,128)(2,1)} %copy-done.2), custom_call_target="tpu_custom_call" | custom-call | flops 1073741824 | bytes 12582912 | tf_op jit(solution)/shard_map/psi_and_density/pallas_call | solution.py:283
  91.8 0.0 copy-done
  91.8 0.0 copy-start.3
  91.8 0.0 copy-done.7
  91.8 0.0 copy-done.8
  91.8 0.0 copy-done.9
  91.9 0.0 copy-done.10
  91.9 0.0 copy-done.11
  91.9 0.0 copy-done.12
  91.9 52.5 %potential_of.1 = (f32[2,128]{1,0:T(2,128)S(1)}, f32[12,2,128]{2,1,0:T(2,128)S(1)}, bf16[8,128,1024]{2,1,0:T(8,128)(2,1)S(1)}, bf16[8,128,1024]{2,1,0:T(8,128)(2,1)S(1)}, bf16[2,4,128,1024]{3,2,1,0:T(8,128)(2,1)}) custom-call(bf16[8,128,1024]{2,1,0:T(8,128)(2,1)S(1)} %get-tuple-element.16.psi.mid, f32[4,2,128]{2,1,0:T(2,128)S(1)} %bitcast.20, ...), custom_call_target="tpu_custom_call" | custom-call | flops 20000000000 | bytes 4000000 | tf_op jit(solution)/shard_map/potential_of/pallas_call | solution.py:444
  144.4 0.0 copy-done.3
  144.4 0.0 copy-start.4
  144.4 1.3 copy-done.4
  145.7 1.4 copy-done.5
  147.1 0.6 copy-done.6
  147.7 20.1 %fock_of.1 = f32[1536,1024]{1,0:T(8,128)} custom-call(s32[24,4]{1,0:T(8,128)} %subtract_bitcast_fusion.lists, bf16[3,8,512,128]{3,2,1,0:T(8,128)(2,1)} %bitcast.15, f32[24,128]{1,0:T(8,128)} %bitcast.17, bf16[8,128,1024]{2,1,0:T(8,128)(2,1)} %copy-done.4, bf16[8,128,1024]{2,1,0:T(8,128)(2,1)} %copy-done.3, bf16[8,128,1024]{2,1,0:T(8,128)(2,1)} %copy-done.5), custom_call_target="tpu_custom_call" | custom-call | tf_op jit(solution)/shard_map/fock_of/pallas_call | solution.py:516
  167.9 0.6 copy.24
  (14 shorter events, 0.1 us)
Async XLA Ops:
  77.7 1.7 copy-start.1
  79.3 1.7 copy-start.2
  81.0 10.8 %copy-start = (bf16[3,4,2,512,128]{4,3,2,1,0:T(8,128)(2,1)}, bf16[3,4,2,512,128]{4,3,2,1,0:T(8,128)(2,1)S(1)}, u32[]{:S(2)}) copy-start(bf16[3,4,2,512,128]{4,3,2,1,0:T(8,128)(2,1)S(1)} %get-tuple-element.13) | copy-start | bytes 9437188
  81.7 10.2 %copy-start.7 = (f32[256]{0:T(256)S(1)}, f32[256]{0:T(256)}, u32[]{:S(2)}) copy-start(f32[256]{0:T(256)} %param.13) | copy-start | bytes 3076
  81.7 10.2 %copy-start.8 = (bf16[2,256,256]{2,1,0:T(8,128)(2,1)S(1)}, bf16[2,256,256]{2,1,0:T(8,128)(2,1)}, u32[]{:S(2)}) copy-start(bf16[2,256,256]{2,1,0:T(8,128)(2,1)} %mw.1) | copy-start | bytes 786436
  81.7 10.2 %copy-start.9 = (bf16[2,256,256]{2,1,0:T(8,128)(2,1)S(1)}, bf16[2,256,256]{2,1,0:T(8,128)(2,1)}, u32[]{:S(2)}) copy-start(bf16[2,256,256]{2,1,0:T(8,128)(2,1)} %aw.1) | copy-start | bytes 786436
  81.7 10.2 %copy-start.10 = (f32[256]{0:T(256)S(1)}, f32[256]{0:T(256)}, u32[]{:S(2)}) copy-start(f32[256]{0:T(256)} %param.15) | copy-start | bytes 3076
  81.7 10.2 %copy-start.11 = (f32[256]{0:T(256)S(1)}, f32[256]{0:T(256)}, u32[]{:S(2)}) copy-start(f32[256]{0:T(256)} %param.16) | copy-start | bytes 3076
  81.7 10.2 %copy-start.12 = (f32[256]{0:T(256)S(1)}, f32[256]{0:T(256)}, u32[]{:S(2)}) copy-start(f32[256]{0:T(256)} %param.19) | copy-start | bytes 3076
  91.8 52.6 %copy-start.3 = (bf16[8,128,1024]{2,1,0:T(8,128)(2,1)}, bf16[8,128,1024]{2,1,0:T(8,128)(2,1)S(1)}, u32[]{:S(2)}) copy-start(bf16[8,128,1024]{2,1,0:T(8,128)(2,1)S(1)} %get-tuple-element.16.psi.mid) | copy-start | bytes 6291460
  144.4 1.3 copy-start.4
  145.7 1.4 copy-start.5
  147.1 0.6 copy-start.6

commit v3 on v2

--- a/solution.py
+++ b/solution.py
@@ -121,7 +121,7 @@
 
 
 def halo_kernel(
-    shape, own, piece, names, low, high, basis, all_names, relay,
+    shape, own, piece, names, low, high, basis, beside, all_names, relay,
     sent, got, passed, piece_sent, piece_got, name_sent, name_got,
 ):
     n_grid, n_atom = shape
@@ -139,31 +139,25 @@
             device_id_type=MESH,
         ).start()
 
+    for r in range(ROUNDS):
+        halo.send(r)
     sides = ((0, 1, grid < n_grid - 1, grid > 0), (2, -1, grid > 0, grid < n_grid - 1))
     for slot, step, able, _ in sides:
 
         @pl.when(able)
         def _():
             send(names, all_names.at[slot], name_sent.at[slot], name_got.at[slot], (grid + step, atom))
-            send(piece, basis.at[slot, atom], piece_sent.at[slot], piece_got.at[slot], (grid + step, atom))
-
-    def to_peers(source, slot, k):
-        @pl.loop(1, n_atom)
-        def _(d):
-            to = lax.rem(atom + d, n_atom)
-            send(source, basis.at[slot, atom], piece_sent.at[k], piece_got.at[k], (grid, to))
-
-    to_peers(piece, 1, 1)
-    for r in range(ROUNDS):
-        halo.send(r)
-    basis[1, atom] = piece[...]
+            send(piece, beside.at[slot // 2], piece_sent.at[slot], piece_got.at[slot], (grid + step, atom))
+
+    basis[atom] = piece[...]
     all_names[1] = names[...]
+
+    @pl.loop(1, n_atom)
+    def _(d):
+        to = lax.rem(atom + d, n_atom)
+        send(piece, basis.at[atom], piece_sent.at[1], piece_got.at[1], (grid, to))
+
     for slot, _, _, filled in sides:
-
-        @pl.when(filled)
-        def _():
-            wait_bytes(piece, piece_got.at[slot])
-            to_peers(basis.at[slot, atom], slot, 3 + slot // 2)
 
         @pl.when(jnp.logical_not(filled))
         def _():
@@ -172,8 +166,8 @@
     for r in range(ROUNDS):
         halo.forward(r)
     peers = pl.ds(0, n_atom - 1)
-    wait_bytes(basis.at[1, peers], piece_got.at[1])
-    wait_bytes(basis.at[1, peers], piece_sent.at[1])
+    wait_bytes(basis.at[peers], piece_got.at[1])
+    wait_bytes(basis.at[peers], piece_sent.at[1])
     for slot, _, able, filled in sides:
 
         @pl.when(able)
@@ -184,8 +178,7 @@
         @pl.when(filled)
         def _():
             wait_bytes(names, name_got.at[slot])
-            wait_bytes(basis.at[slot, peers], piece_got.at[3 + slot // 2])
-            wait_bytes(basis.at[slot, peers], piece_sent.at[3 + slot // 2])
+            wait_bytes(piece, piece_got.at[slot])
 
     halo.finish()
 
@@ -198,21 +191,22 @@
         out_shape=(
             jax.ShapeDtypeStruct(own.shape, own.dtype),
             jax.ShapeDtypeStruct(own.shape, own.dtype),
-            jax.ShapeDtypeStruct((3, shape[1], *piece.shape), piece.dtype),
+            jax.ShapeDtypeStruct((shape[1], *piece.shape), piece.dtype),
+            jax.ShapeDtypeStruct((2, *piece.shape), piece.dtype),
             jax.ShapeDtypeStruct((3, *names.shape), names.dtype),
             jax.ShapeDtypeStruct((2, rows // 2, columns), own.dtype),
         ),
         in_specs=[anywhere, VMEM, VMEM],
-        out_specs=(anywhere, anywhere, VMEM, VMEM, anywhere),
+        out_specs=(anywhere, anywhere, VMEM, VMEM, VMEM, anywhere),
         scratch_shapes=halo_scratch(ROUNDS)
         + [
-            pltpu.SemaphoreType.DMA((5,)),
-            pltpu.SemaphoreType.DMA((5,)),
+            pltpu.SemaphoreType.DMA((3,)),
+            pltpu.SemaphoreType.DMA((3,)),
             pltpu.SemaphoreType.DMA((3,)),
             pltpu.SemaphoreType.DMA((3,)),
         ],
         compiler_params=pltpu.CompilerParams(
-            collective_id=1, has_side_effects=True, vmem_limit_bytes=40 << 20
+            collective_id=1, has_side_effects=True, vmem_limit_bytes=20 << 20
         ),
         name="halo_of",
     )(own, piece, names)
@@ -249,7 +243,7 @@
     def _():
         sums[...] = jnp.zeros_like(sums)
         for b in range(count):
-            basis[b] = jnp.transpose(basis_t[0, b])
+            basis[b] = jnp.transpose(basis_t[b])
 
     @pl.loop(0, count)
     def _(b):
@@ -277,8 +271,9 @@
 
 def psi_and_density(lists, basis_t, below, own, above):
     owned, columns = own.shape
-    _, count, depth, points = basis_t.shape
-    wide = min(columns, 256)
+    count, depth, points = basis_t.shape
+    wide = min(columns, 512)
+    grant = 2 * (9 * owned * wide + 2 * count * points * wide + 4 * count * depth * points)
     tile = pl.BlockSpec((owned, wide), lambda i, lists: (0, i))
     return pl.pallas_call(
         psi_kernel,
@@ -290,7 +285,7 @@
             num_scalar_prefetch=1,
             grid=(columns // wide,),
             in_specs=[
-                pl.BlockSpec((1, count, depth, points), lambda i, lists: (1, 0, 0, 0)),
+                pl.BlockSpec((count, depth, points), lambda i, lists: (0, 0, 0)),
                 tile,
                 tile,
                 tile,
@@ -305,7 +300,7 @@
                 pltpu.VMEM((count, points, depth), jnp.bfloat16),
             ],
         ),
-        compiler_params=pltpu.CompilerParams(vmem_limit_bytes=48 << 20),
+        compiler_params=pltpu.CompilerParams(vmem_limit_bytes=grant + (6 << 20)),
         cost_estimate=pl.CostEstimate(
             flops=2 * count * points * depth * columns,
             bytes_accessed=8 * owned * columns,
@@ -316,10 +311,10 @@
 
 
 def potential_kernel(
-    shape, layers, psi, dens, info, mine, hot, hot_t, weights, scale, shift, mw, aw, head,
-    pot, near, psi_low, psi_high, relay,
+    shape, layers, psi, beside, dens, info, mine, hot, hot_t, weights, scale, shift, mw, aw, head,
+    pot, near, psi_low, psi_high, relay, beside_t,
     dens_buf, info_buf, rows_out, rows_buf, scaled_out, scaled_buf, sent, got,
-    psi_sent, psi_got, psi_passed,
+    psi_sent, psi_got, psi_passed, piece_sent, piece_got,
 ):
     n_grid, n_atom = shape
     n = n_grid * n_atom
@@ -363,6 +358,21 @@
 
     to_all(info, info_buf, 1)
     halo.send(0)
+    for slot in range(2):
+        beside_t[slot, atom] = beside[slot]
+
+        @pl.loop(1, n_atom)
+        def _(d):
+            to = lax.rem(atom + d, n_atom)
+            pltpu.make_async_remote_copy(
+                src_ref=beside.at[slot],
+                dst_ref=beside_t.at[slot, atom],
+                send_sem=piece_sent.at[slot],
+                recv_sem=piece_got.at[slot],
+                device_id=(grid, to),
+                device_id_type=MESH,
+            ).start()
+
     dens_buf[atom] = dens[atom]
     info_buf[me] = info[...]
     weight = to_columns(weights[...])[:, 0:1]
@@ -432,10 +442,13 @@
     for layer in range(layers):
         wait_all(rows_buf.at[layer], sent.at[2 + layer], n - 1)
     wait_all(scaled_buf, sent.at[last], n - 1)
+    for slot in range(2):
+        wait_all(beside_t.at[slot], piece_got.at[slot], n_atom - 1)
+        wait_all(beside_t.at[slot], piece_sent.at[slot], n_atom - 1)
     halo.finish()
 
 
-def potential_of(shape, psi, dens, info, mine, hot, hot_t, weights, scale, shift, mw, aw, head):
+def potential_of(shape, psi, beside, dens, info, mine, hot, hot_t, weights, scale, shift, mw, aw, head):
     n_atom, batches, points = dens.shape
     n = shape[0] * shape[1]
     layers, features, _ = mw.shape
@@ -449,9 +462,10 @@
             jax.ShapeDtypeStruct(psi.shape, psi.dtype),
             jax.ShapeDtypeStruct(psi.shape, psi.dtype),
             jax.ShapeDtypeStruct((2, psi.shape[0] // 2, *psi.shape[1:]), psi.dtype),
-        ),
-        in_specs=[anywhere] + [VMEM] * 11,
-        out_specs=(VMEM, VMEM, anywhere, anywhere, anywhere),
+            jax.ShapeDtypeStruct((2, n_atom, *beside.shape[1:]), beside.dtype),
+        ),
+        in_specs=[anywhere] + [VMEM] * 12,
+        out_specs=(VMEM, VMEM, anywhere, anywhere, anywhere, VMEM),
         scratch_shapes=[
             pltpu.VMEM((n_atom, batches, points), jnp.float32),
             pltpu.VMEM((n, RUN, LANES), jnp.float32),
@@ -462,32 +476,32 @@
             pltpu.SemaphoreType.DMA((3 + layers,)),
             pltpu.SemaphoreType.DMA((3 + layers,)),
         ]
-        + halo_scratch(layers + 2),
+        + halo_scratch(layers + 2)
+        + [pltpu.SemaphoreType.DMA((2,)), pltpu.SemaphoreType.DMA((2,))],
         compiler_params=pltpu.CompilerParams(
-            collective_id=0, has_side_effects=True, vmem_limit_bytes=32 << 20
+            collective_id=0, has_side_effects=True, vmem_limit_bytes=30 << 20
         ),
         cost_estimate=pl.CostEstimate(
             flops=20_000_000_000, bytes_accessed=4_000_000, transcendentals=0
         ),
         name="potential_of",
-    )(psi, dens, info, mine, hot, hot_t, weights, scale, shift, mw, aw, head)
-
-
-def fock_kernel(lists, basis_t, near, low, mid, high, out, scaled):
+    )(psi, beside, dens, info, mine, hot, hot_t, weights, scale, shift, mw, aw, head)
+
+
+def fock_kernel(lists, own_t, beside_t, near, low, mid, high, out, scaled):
     step = pl.program_id(0)
-    groups, count, depth, points = basis_t.shape
+    groups, count, depth, points = scaled.shape
     picks = lists.shape[1]
     width = depth // picks
     owned = out.shape[0] // width
 
     @pl.when(step == 0)
     def _():
-        @pl.loop(0, groups)
-        def _(k):
-            @pl.loop(0, count)
-            def _(b):
+        @pl.loop(0, count)
+        def _(b):
+            for k, values in enumerate((beside_t.at[0], own_t, beside_t.at[1])):
                 scaled[k, b] = (
-                    basis_t[k, b].astype(jnp.float32) * near[pl.ds(k * count + b, 1), :]
+                    values[b].astype(jnp.float32) * near[pl.ds(k * count + b, 1), :]
                 ).astype(jnp.bfloat16)
 
     out[...] = jnp.zeros_like(out)
@@ -508,11 +522,13 @@
                     )
 
 
-def fock_of(lists, basis_t, near, low, mid, high, owned):
-    groups, count, depth, points = basis_t.shape
+def fock_of(lists, own_t, beside_t, near, low, mid, high, owned):
+    count, depth, points = own_t.shape
+    groups = 3
     columns = mid.shape[2]
     wide = min(columns, 512)
     tile = pl.BlockSpec((count, points, wide), lambda i, lists: (0, 0, i))
+    grant = 2 * (9 * count * depth * points + 6 * count * points * wide + 4 * owned * wide)
     return pl.pallas_call(
         fock_kernel,
         out_shape=jax.ShapeDtypeStruct((owned, columns), jnp.float32),
@@ -520,7 +536,8 @@
             num_scalar_prefetch=1,
             grid=(columns // wide,),
             in_specs=[
-                pl.BlockSpec((groups, count, depth, points), lambda i, lists: (0, 0, 0, 0)),
+                pl.BlockSpec((count, depth, points), lambda i, lists: (0, 0, 0)),
+                pl.BlockSpec((2, count, depth, points), lambda i, lists: (0, 0, 0, 0)),
                 pl.BlockSpec((groups * count, points), lambda i, lists: (0, 0)),
                 tile,
                 tile,
@@ -529,9 +546,9 @@
             out_specs=pl.BlockSpec((owned, wide), lambda i, lists: (0, i)),
             scratch_shapes=[pltpu.VMEM((groups, count, depth, points), jnp.bfloat16)],
         ),
-        compiler_params=pltpu.CompilerParams(vmem_limit_bytes=60 << 20),
+        compiler_params=pltpu.CompilerParams(vmem_limit_bytes=grant + (4 << 20)),
         name="fock_of",
-    )(lists, basis_t, near, low, mid, high)
+    )(lists, own_t, beside_t, near, low, mid, high)
 
 
 def local(
@@ -554,10 +571,10 @@
     shape = (n_grid, n_atom)
     first = lax.axis_index("grid") * owned
     names = jnp.pad(block_lists, ((0, 0), (0, LANES - block_lists.shape[1])))
-    below, above, basis_t, names, _ = halo_of(
+    below, above, own_t, beside, names, _ = halo_of(
         shape, orbitals, jnp.swapaxes(basis_values, 1, 2), names
     )
-    basis_t = basis_t.reshape(3, n_atom * batches, depth, points)
+    own_t = own_t.reshape(n_atom * batches, depth, points)
     lists = names[:, :, : block_lists.shape[1]].reshape(-1, block_lists.shape[1]) - first
 
     total = ATOM_DEV * n_atom
@@ -575,10 +592,11 @@
     mine = jnp.where(lanes < RUN, names, -1.0)[None, :]
     info = jnp.where(lanes[None, :] < LANES // 2, names[:RUN, None], mass[:, None])
 
-    psi, dens = psi_and_density(block_lists - first + owned, basis_t, below, orbitals, above)
-    potential, near, psi_low, psi_high, _ = potential_of(
+    psi, dens = psi_and_density(block_lists - first + owned, own_t, below, orbitals, above)
+    potential, near, psi_low, psi_high, _, beside_t = potential_of(
         shape,
         psi,
+        beside,
         dens.reshape(n_atom, batches, points),
         info,
         mine,
@@ -592,7 +610,8 @@
         head_weight[None, :],
     )
     fock = fock_of(
-        lists, basis_t, near.reshape(-1, points), psi_low, psi, psi_high, own_rows
+        lists, own_t, beside_t.reshape(2, *own_t.shape), near.reshape(-1, points),
+        psi_low, psi, psi_high, own_rows,
     )
     return (fock, potential.reshape(-1))
 

time: 169 us -> 182 us (1.077); the launches traced: 168 us -> 179 us
  Pallas kernels: 152 us -> 168 us
  local copies, waits for them, and re-layouts: 10.3 us -> 5.56 us
    pallas_call x1, Pallas kernels: 52.5 us -> 97.5 us  [potential_of(): pl.pallas_call(functools.partial(potential_kernel, shape, layers), out_sh...]
    pallas_call x1, Pallas kernels: 68.9 us -> 49 us  [halo_of(): pl.pallas_call(functools.partial(halo_kernel, shape), out_shape=(jax.Shap...]
    pallas_call x1, Pallas kernels: 20.1 us -> 15.1 us  [fock_of(): pl.pallas_call(fock_kernel, out_shape=jax.ShapeDtypeStruct((owned, column...]
    unnamed x29 -> x19, local copies, waits for them, and re-layouts: 9.14 us -> 4.37 us
    pallas_call x1, Pallas kernels: 10.1 us -> 6.56 us  [psi_and_density(): pl.pallas_call(psi_kernel, out_shape=(jax.ShapeDtypeStruct((count, points...]
where the time goes in v3:
time: 182 us; the launch traced here: 179 us
  Pallas kernels  168 us (92%)
  local copies, waits for them, and re-layouts  5.56 us (3%)
  other arithmetic  3.67 us (2%)
  between operations  2.13 us (1%)
    pallas_call x1, Pallas kernels, potential_of(): pl.pallas_call(functools.partial(potential_kernel, shape, layers), out_sh...  97.5 us
    pallas_call x1, Pallas kernels, halo_of(): pl.pallas_call(functools.partial(halo_kernel, shape), out_shape=(jax.Shap...  49 us
    pallas_call x1, Pallas kernels, fock_of(): pl.pallas_call(fock_kernel, out_shape=jax.ShapeDtypeStruct((owned, column...  15.1 us
    pallas_call x1, Pallas kernels, psi_and_density(): pl.pallas_call(psi_kernel, out_shape=(jax.ShapeDtypeStruct((count, points...  6.56 us
    unnamed x19, local copies, waits for them, and re-layouts  4.37 us

profile of v3, /device:TPU:4, one launch (start us, length us, event | category | flops | bytes accessed | tf_op | source)
XLA Modules:
  0.0 179.5 jit_solution(28338419717236659)
XLA Ops:
  0.6 1.2 slice.13
  1.8 2.0 %fusion.8 = (s32[]{:T(128)}, s32[256]{0:T(256)S(1)}) fusion(s32[256]{0:T(256)} %param.14, s32[]{:T(128)} %bitcast.4), kind=kLoop, calls=%fused_computation.26 | loop fusion | flops 3839 | bytes 2056 | tf_op jit(solution)/shard_map/reduce_min | solution.py:583
  5.1 0.7 broadcast_subtract_fusion
  5.8 0.8 select_reduce_fusion
  6.6 0.1 broadcast_select_fusion.info
  6.7 0.8 copy.18
  7.5 0.1 fusion.hot
  7.6 1.1 copy.17
  8.7 0.0 copy-start
  8.7 1.9 %copy-done = bf16[1536,1024]{1,0:T(8,128)(2,1)S(1)} copy-done((bf16[1536,1024]{1,0:T(8,128)(2,1)S(1)}, bf16[1536,1024]{1,0:T(8,128)(2,1)}, u32[]{:S(2)}) %copy-start) | copy-done | bytes 3145752
  10.6 0.0 copy-start.1
  10.6 49.0 %halo_of.1 = (bf16[1536,1024]{1,0:T(8,128)(2,1)S(1)}, bf16[1536,1024]{1,0:T(8,128)(2,1)S(1)}, bf16[4,2,512,128]{3,2,1,0:T(8,128)(2,1)S(1)}, bf16[2,2,512,128]{3,...) custom-call(bf16[1536,1024]{1,0:T(8,128)(2,1)S(1)} %copy-done, ...), custom_call_target="tpu_custom_call" | custom-call | tf_op jit(solution)/shard_map/halo_of/pallas_call | solution.py:189
  59.6 0.0 copy-done.1
  59.6 0.0 copy-start.2
  59.6 0.0 copy-start.3
  59.6 0.0 copy-start.4
  59.6 0.0 copy-start.5
  59.7 0.0 copy-start.6
  59.7 0.0 copy-start.7
  59.7 6.6 %psi_and_density.1 = (bf16[8,128,1024]{2,1,0:T(8,128)(2,1)S(1)}, f32[8,128]{1,0:T(8,128)S(1)}) custom-call(s32[8,4]{1,0:T(8,128)S(1)} %subtract_add_fusion.lists, bf16[8,512,128]{2,1,0:T(8,128)(2,1)S(1)} %bitcast.15, bf16[1536,1024]{1,0:T(8,128)(2,1)S(1)} %get-tuple-element.16.below, bf16[1536,1024]{1,0:T(8,128)(2,1)S(1)} %copy-done.1, ...), custom_call_target="tpu_custom_call" | custom-call | flops 1073741824 | bytes 12582912 | tf_op jit(solution)/shard_map/psi_and_density/pallas_call | solution.py:278
  66.3 0.0 copy-done.2
  66.3 0.0 copy-done.3
  66.3 0.0 copy-done.4
  66.3 0.0 copy-done.5
  66.3 0.0 copy-done.6
  66.3 0.0 copy-done.7
  66.3 97.5 %potential_of.1 = (f32[2,128]{1,0:T(2,128)S(1)}, f32[12,2,128]{2,1,0:T(2,128)S(1)}, bf16[8,128,1024]{2,1,0:T(8,128)(2,1)S(1)}, bf16[8,128,1024]{2,1,0:T(8,128)(2...) custom-call(bf16[8,128,1024]{2,1,0:T(8,128)(2,1)S(1)} %get-tuple-element.18.psi.mid, ...), custom_call_target="tpu_custom_call" | custom-call | flops 20000000000 | bytes 4000000 | tf_op jit(solution)/shard_map/potential_of/pallas_call | solution.py:457
  163.8 15.1 %fock_of.1 = f32[1536,1024]{1,0:T(8,128)} custom-call(s32[24,4]{1,0:T(8,128)S(1)} %subtract_bitcast_fusion.lists, bf16[8,512,128]{2,1,0:T(8,128)(2,1)S(1)} %bitcast.16, bf16[2,8,512,128]{3,2,1,0:T(8,128)(2,1)S(1)} %bitcast.17, f32[24,128]{1,0:T(8,128)S(1)} %bitcast.19, bf16[8,128,1024]{2,1,0:T(8,128)(2,1)S(1)} %get-tuple-element.23.low, ...), custom_call_target="tpu_custom_call" | custom-call | tf_op jit(solution)/shard_map/fock_of/pallas_call | solution.py:532
  178.9 0.6 copy.24
  (7 shorter events, 0.1 us)
Async XLA Ops:
  8.7 1.9 %copy-start = (bf16[1536,1024]{1,0:T(8,128)(2,1)S(1)}, bf16[1536,1024]{1,0:T(8,128)(2,1)}, u32[]{:S(2)}) copy-start(bf16[1536,1024]{1,0:T(8,128)(2,1)} %own.3) | copy-start | bytes 9437188
  10.6 49.0 %copy-start.1 = (bf16[1536,1024]{1,0:T(8,128)(2,1)S(1)}, bf16[1536,1024]{1,0:T(8,128)(2,1)}, u32[]{:S(2)}) copy-start(bf16[1536,1024]{1,0:T(8,128)(2,1)} %own.3) | copy-start | bytes 9437188
  59.6 6.6 %copy-start.2 = (f32[256]{0:T(256)S(1)}, f32[256]{0:T(256)}, u32[]{:S(2)}) copy-start(f32[256]{0:T(256)} %param.13) | copy-start | bytes 3076
  59.6 6.6 %copy-start.3 = (bf16[2,256,256]{2,1,0:T(8,128)(2,1)S(1)}, bf16[2,256,256]{2,1,0:T(8,128)(2,1)}, u32[]{:S(2)}) copy-start(bf16[2,256,256]{2,1,0:T(8,128)(2,1)} %mw.1) | copy-start | bytes 786436
  59.6 6.6 %copy-start.4 = (bf16[2,256,256]{2,1,0:T(8,128)(2,1)S(1)}, bf16[2,256,256]{2,1,0:T(8,128)(2,1)}, u32[]{:S(2)}) copy-start(bf16[2,256,256]{2,1,0:T(8,128)(2,1)} %aw.1) | copy-start | bytes 786436
  59.6 6.6 %copy-start.5 = (f32[256]{0:T(256)S(1)}, f32[256]{0:T(256)}, u32[]{:S(2)}) copy-start(f32[256]{0:T(256)} %param.15) | copy-start | bytes 3076
  59.7 6.6 %copy-start.6 = (f32[256]{0:T(256)S(1)}, f32[256]{0:T(256)}, u32[]{:S(2)}) copy-start(f32[256]{0:T(256)} %param.16) | copy-start | bytes 3076
  59.7 6.6 %copy-start.7 = (f32[256]{0:T(256)S(1)}, f32[256]{0:T(256)}, u32[]{:S(2)}) copy-start(f32[256]{0:T(256)} %param.19) | copy-start | bytes 3076

commit v4 on v2

--- a/solution.py
+++ b/solution.py
@@ -122,7 +122,7 @@
 
 def halo_kernel(
     shape, own, piece, names, low, high, basis, all_names, relay,
-    sent, got, passed, piece_sent, piece_got, name_sent, name_got,
+    sent, got, passed, piece_sent, piece_got, name_sent, name_got, line_sent, line_got,
 ):
     n_grid, n_atom = shape
     grid, atom = lax.axis_index("grid"), lax.axis_index("atom")
@@ -147,15 +147,44 @@
             send(names, all_names.at[slot], name_sent.at[slot], name_got.at[slot], (grid + step, atom))
             send(piece, basis.at[slot, atom], piece_sent.at[slot], piece_got.at[slot], (grid + step, atom))
 
-    def to_peers(source, slot, k):
-        @pl.loop(1, n_atom)
-        def _(d):
-            to = lax.rem(atom + d, n_atom)
-            send(source, basis.at[slot, atom], piece_sent.at[k], piece_got.at[k], (grid, to))
-
-    to_peers(piece, 1, 1)
     for r in range(ROUNDS):
         halo.send(r)
+
+    def line(slot, d, way):
+        origin = atom - (d - 1) if way == 0 else atom + (d - 1)
+        able = (
+            jnp.logical_and(atom < n_atom - 1, atom >= d - 1)
+            if way == 0
+            else jnp.logical_and(atom > 0, atom + d - 1 < n_atom)
+        )
+        return jnp.clip(origin, 0, n_atom - 1), able
+
+    filled_of = {0: grid > 0, 1: grid >= 0, 2: grid < n_grid - 1}
+
+    def line_send(slot, d):
+        for way in range(2):
+            origin, able = line(slot, d, way)
+
+            @pl.when(jnp.logical_and(able, filled_of[slot]))
+            def _():
+                source = piece if slot == 1 and d == 1 else basis.at[slot, origin]
+                send(
+                    source, basis.at[slot, origin], line_sent.at[slot, way, d - 1],
+                    line_got.at[slot, way, d - 1], (grid, atom + 1 - 2 * way),
+                )
+
+    def line_wait(slot, d, sems, arrived):
+        for way in range(2):
+            if arrived:
+                able = atom >= d if way == 0 else atom + d < n_atom
+            else:
+                able = line(slot, d, way)[1]
+
+            @pl.when(jnp.logical_and(able, filled_of[slot]))
+            def _():
+                wait_bytes(piece, sems.at[slot, way, d - 1])
+
+    line_send(1, 1)
     basis[1, atom] = piece[...]
     all_names[1] = names[...]
     for slot, _, _, filled in sides:
@@ -163,17 +192,25 @@
         @pl.when(filled)
         def _():
             wait_bytes(piece, piece_got.at[slot])
-            to_peers(basis.at[slot, atom], slot, 3 + slot // 2)
 
         @pl.when(jnp.logical_not(filled))
         def _():
             all_names[slot] = jnp.full_like(names, -1)
 
-    for r in range(ROUNDS):
-        halo.forward(r)
-    peers = pl.ds(0, n_atom - 1)
-    wait_bytes(basis.at[1, peers], piece_got.at[1])
-    wait_bytes(basis.at[1, peers], piece_sent.at[1])
+    line_send(0, 1)
+    line_send(2, 1)
+    moved = 0
+    for d in range(1, n_atom):
+        for slot in (1, 0, 2):
+            line_wait(slot, d, line_got, True)
+            if d < n_atom - 1:
+                line_send(slot, d + 1)
+        while moved < ROUNDS and moved < (d * ROUNDS) // (n_atom - 1):
+            halo.forward(moved)
+            moved += 1
+    for d in range(1, n_atom):
+        for slot in (1, 0, 2):
+            line_wait(slot, d, line_sent, False)
     for slot, _, able, filled in sides:
 
         @pl.when(able)
@@ -184,8 +221,6 @@
         @pl.when(filled)
         def _():
             wait_bytes(names, name_got.at[slot])
-            wait_bytes(basis.at[slot, peers], piece_got.at[3 + slot // 2])
-            wait_bytes(basis.at[slot, peers], piece_sent.at[3 + slot // 2])
 
     halo.finish()
 
@@ -206,13 +241,15 @@
         out_specs=(anywhere, anywhere, VMEM, VMEM, anywhere),
         scratch_shapes=halo_scratch(ROUNDS)
         + [
-            pltpu.SemaphoreType.DMA((5,)),
-            pltpu.SemaphoreType.DMA((5,)),
             pltpu.SemaphoreType.DMA((3,)),
             pltpu.SemaphoreType.DMA((3,)),
+            pltpu.SemaphoreType.DMA((3,)),
+            pltpu.SemaphoreType.DMA((3,)),
+            pltpu.SemaphoreType.DMA((3, 2, shape[1] - 1)),
+            pltpu.SemaphoreType.DMA((3, 2, shape[1] - 1)),
         ],
         compiler_params=pltpu.CompilerParams(
-            collective_id=1, has_side_effects=True, vmem_limit_bytes=40 << 20
+            collective_id=1, has_side_effects=True, vmem_limit_bytes=24 << 20
         ),
         name="halo_of",
     )(own, piece, names)
@@ -278,7 +315,8 @@
 def psi_and_density(lists, basis_t, below, own, above):
     owned, columns = own.shape
     _, count, depth, points = basis_t.shape
-    wide = min(columns, 256)
+    wide = min(columns, 512)
+    grant = 2 * (9 * owned * wide + 2 * count * points * wide + 4 * count * depth * points)
     tile = pl.BlockSpec((owned, wide), lambda i, lists: (0, i))
     return pl.pallas_call(
         psi_kernel,
@@ -305,7 +343,7 @@
                 pltpu.VMEM((count, points, depth), jnp.bfloat16),
             ],
         ),
-        compiler_params=pltpu.CompilerParams(vmem_limit_bytes=48 << 20),
+        compiler_params=pltpu.CompilerParams(vmem_limit_bytes=grant + (6 << 20)),
         cost_estimate=pl.CostEstimate(
             flops=2 * count * points * depth * columns,
             bytes_accessed=8 * owned * columns,
@@ -464,7 +502,7 @@
         ]
         + halo_scratch(layers + 2),
         compiler_params=pltpu.CompilerParams(
-            collective_id=0, has_side_effects=True, vmem_limit_bytes=32 << 20
+            collective_id=0, has_side_effects=True, vmem_limit_bytes=24 << 20
         ),
         cost_estimate=pl.CostEstimate(
             flops=20_000_000_000, bytes_accessed=4_000_000, transcendentals=0
@@ -513,6 +551,7 @@
     columns = mid.shape[2]
     wide = min(columns, 512)
     tile = pl.BlockSpec((count, points, wide), lambda i, lists: (0, 0, i))
+    grant = 2 * (9 * count * depth * points + 6 * count * points * wide + 4 * owned * wide)
     return pl.pallas_call(
         fock_kernel,
         out_shape=jax.ShapeDtypeStruct((owned, columns), jnp.float32),
@@ -529,7 +568,7 @@
             out_specs=pl.BlockSpec((owned, wide), lambda i, lists: (0, i)),
             scratch_shapes=[pltpu.VMEM((groups, count, depth, points), jnp.bfloat16)],
         ),
-        compiler_params=pltpu.CompilerParams(vmem_limit_bytes=60 << 20),
+        compiler_params=pltpu.CompilerParams(vmem_limit_bytes=grant + (4 << 20)),
         name="fock_of",
     )(lists, basis_t, near, low, mid, high)
 

time: 169 us -> 144 us (0.85)
  Pallas kernels: 152 us -> 132 us
  local copies, waits for them, and re-layouts: 10.3 us -> 5.56 us
    pallas_call x1, Pallas kernels: 68.9 us -> 57.6 us  [halo_of(): pl.pallas_call(functools.partial(halo_kernel, shape), out_shape=(jax.Shap...]
    unnamed x29 -> x19, local copies, waits for them, and re-layouts: 9.14 us -> 4.37 us
    pallas_call x1, Pallas kernels: 20.1 us -> 16.6 us  [fock_of(): pl.pallas_call(fock_kernel, out_shape=jax.ShapeDtypeStruct((owned, column...]
    pallas_call x1, Pallas kernels: 10.1 us -> 6.57 us  [psi_and_density(): pl.pallas_call(psi_kernel, out_shape=(jax.ShapeDtypeStruct((count, points...]
where the time goes in v4:
time: 144 us; the launch traced here: 143 us
  Pallas kernels  132 us (92%)
  local copies, waits for them, and re-layouts  5.56 us (4%)
  other arithmetic  3.67 us (3%)
  between operations  2.13 us (1%)
    pallas_call x1, Pallas kernels, halo_of(): pl.pallas_call(functools.partial(halo_kernel, shape), out_shape=(jax.Shap...  57.6 us
    pallas_call x1, Pallas kernels, potential_of(): pl.pallas_call(functools.partial(potential_kernel, shape, layers), out_sh...  50.8 us
    pallas_call x1, Pallas kernels, fock_of(): pl.pallas_call(fock_kernel, out_shape=jax.ShapeDtypeStruct((owned, column...  16.6 us
    pallas_call x1, Pallas kernels, psi_and_density(): pl.pallas_call(psi_kernel, out_shape=(jax.ShapeDtypeStruct((count, points...  6.57 us
    unnamed x19, local copies, waits for them, and re-layouts  4.37 us

profile of v4, /device:TPU:4, one launch (start us, length us, event | category | flops | bytes accessed | tf_op | source)
XLA Modules:
  0.0 142.9 jit_solution(11056430502375952635)
XLA Ops:
  0.6 1.2 slice.13
  1.8 2.0 %fusion.8 = (s32[]{:T(128)}, s32[256]{0:T(256)S(1)}) fusion(s32[256]{0:T(256)} %param.14, s32[]{:T(128)} %bitcast.4), kind=kLoop, calls=%fused_computation.26 | loop fusion | flops 3839 | bytes 2056 | tf_op jit(solution)/shard_map/reduce_min | solution.py:605
  5.1 0.7 broadcast_subtract_fusion
  5.8 0.8 select_reduce_fusion
  6.6 0.1 broadcast_select_fusion.info
  6.7 0.8 copy.18
  7.5 0.1 fusion.hot
  7.6 1.1 copy.17
  8.7 0.0 copy-start
  8.7 1.9 %copy-done = bf16[1536,1024]{1,0:T(8,128)(2,1)S(1)} copy-done((bf16[1536,1024]{1,0:T(8,128)(2,1)S(1)}, bf16[1536,1024]{1,0:T(8,128)(2,1)}, u32[]{:S(2)}) %copy-start) | copy-done | bytes 3145752
  10.6 0.0 copy-start.1
  10.6 57.6 %halo_of.1 = (bf16[1536,1024]{1,0:T(8,128)(2,1)S(1)}, bf16[1536,1024]{1,0:T(8,128)(2,1)S(1)}, bf16[3,4,2,512,128]{4,3,2,1,0:T(8,128)(2,1)S(1)}, s32[3,8,128]{2,1,0:T(8,128)S(1)}, bf16[2,768,1024]{2,1,0:T(8,128)(2,1)}) custom-call(bf16[1536,1024]{1,0:T(8,128)(2,1)S(1)} %copy-done, bf16[2,512,128]{2,1,0:T(8,128)(2,1)S(1)} %bitcast.16, s32[8,128]{1,0:T(8,128)S(1)} %pad.4.names), custom_call_target="tpu_custom_call" | custom-call | tf_op jit(solution)/shard_map/halo_of/pallas_call | solution.py:231
  68.2 0.0 copy-done.1
  68.2 0.0 copy-start.2
  68.2 0.0 copy-start.3
  68.2 0.0 copy-start.4
  68.3 0.0 copy-start.5
  68.3 0.0 copy-start.6
  68.3 0.0 copy-start.7
  68.3 6.6 %psi_and_density.1 = (bf16[8,128,1024]{2,1,0:T(8,128)(2,1)S(1)}, f32[8,128]{1,0:T(8,128)S(1)}) custom-call(s32[8,4]{1,0:T(8,128)S(1)} %subtract_add_fusion.lists, bf16[3,8,512,128]{3,2,1,0:T(8,128)(2,1)S(1)} %bitcast.14, bf16[1536,1024]{1,0:T(8,128)(2,1)S(1)} %get-tuple-element.14.below, bf16[1536,1024]{1,0:T(8,128)(2,1)S(1)} %copy-done.1, ...), custom_call_target="tpu_custom_call" | custom-call | flops 1073741824 | bytes 12582912 | tf_op jit(solution)/shard_map/psi_and_density/pallas_call | solution.py:321
  74.9 0.0 copy-done.2
  74.9 0.0 copy-done.3
  74.9 0.0 copy-done.4
  74.9 0.0 copy-done.5
  74.9 0.0 copy-done.6
  74.9 0.0 copy-done.7
  74.9 50.8 %potential_of.1 = (f32[2,128]{1,0:T(2,128)S(1)}, f32[12,2,128]{2,1,0:T(2,128)S(1)}, bf16[8,128,1024]{2,1,0:T(8,128)(2,1)S(1)}, bf16[8,128,1024]{2,1,0:T(8,128)(2,1)S(1)}, bf16[2,4,128,1024]{3,2,1,0:T(8,128)(2,1)}) custom-call(bf16[8,128,1024]{2,1,0:T(8,128)(2,1)S(1)} %get-tuple-element.16.psi.mid, f32[4,2,128]{2,1,0:T(2,128)S(1)} %bitcast.20, ...), custom_call_target="tpu_custom_call" | custom-call | flops 20000000000 | bytes 4000000 | tf_op jit(solution)/shard_map/potential_of/pallas_call | solution.py:482
  125.8 16.6 %fock_of.1 = f32[1536,1024]{1,0:T(8,128)} custom-call(s32[24,4]{1,0:T(8,128)S(1)} %subtract_bitcast_fusion.lists, bf16[3,8,512,128]{3,2,1,0:T(8,128)(2,1)S(1)} %bitcast.15, f32[24,128]{1,0:T(8,128)S(1)} %bitcast.17, bf16[8,128,1024]{2,1,0:T(8,128)(2,1)S(1)} %get-tuple-element.19.low, bf16[8,128,1024]{2,1,0:T(8,128)(2,1)S(1)} %get-tuple-element.16.psi.mid, ...), custom_call_target="tpu_custom_call" | custom-call | tf_op jit(solution)/shard_map/fock_of/pallas_call | solution.py:555
  142.3 0.6 copy.24
  (7 shorter events, 0.1 us)
Async XLA Ops:
  8.7 1.9 %copy-start = (bf16[1536,1024]{1,0:T(8,128)(2,1)S(1)}, bf16[1536,1024]{1,0:T(8,128)(2,1)}, u32[]{:S(2)}) copy-start(bf16[1536,1024]{1,0:T(8,128)(2,1)} %own.3) | copy-start | bytes 9437188
  10.6 57.6 %copy-start.1 = (bf16[1536,1024]{1,0:T(8,128)(2,1)S(1)}, bf16[1536,1024]{1,0:T(8,128)(2,1)}, u32[]{:S(2)}) copy-start(bf16[1536,1024]{1,0:T(8,128)(2,1)} %own.3) | copy-start | bytes 9437188
  68.2 6.6 %copy-start.2 = (f32[256]{0:T(256)S(1)}, f32[256]{0:T(256)}, u32[]{:S(2)}) copy-start(f32[256]{0:T(256)} %param.13) | copy-start | bytes 3076
  68.2 6.6 %copy-start.3 = (bf16[2,256,256]{2,1,0:T(8,128)(2,1)S(1)}, bf16[2,256,256]{2,1,0:T(8,128)(2,1)}, u32[]{:S(2)}) copy-start(bf16[2,256,256]{2,1,0:T(8,128)(2,1)} %mw.1) | copy-start | bytes 786436
  68.2 6.6 %copy-start.4 = (bf16[2,256,256]{2,1,0:T(8,128)(2,1)S(1)}, bf16[2,256,256]{2,1,0:T(8,128)(2,1)}, u32[]{:S(2)}) copy-start(bf16[2,256,256]{2,1,0:T(8,128)(2,1)} %aw.1) | copy-start | bytes 786436
  68.3 6.6 %copy-start.5 = (f32[256]{0:T(256)S(1)}, f32[256]{0:T(256)}, u32[]{:S(2)}) copy-start(f32[256]{0:T(256)} %param.15) | copy-start | bytes 3076
  68.3 6.6 %copy-start.6 = (f32[256]{0:T(256)S(1)}, f32[256]{0:T(256)}, u32[]{:S(2)}) copy-start(f32[256]{0:T(256)} %param.16) | copy-start | bytes 3076
  68.3 6.6 %copy-start.7 = (f32[256]{0:T(256)S(1)}, f32[256]{0:T(256)}, u32[]{:S(2)}) copy-start(f32[256]{0:T(256)} %param.19) | copy-start | bytes 3076

commit v5 on v4

--- a/solution.py
+++ b/solution.py
@@ -424,6 +424,8 @@
         ).astype(jnp.bfloat16)
         to_all(rows_out.at[layer], rows_buf.at[layer], 2 + layer)
         halo.send(1 + layer)
+        if layer == 0:
+            halo.send(layers + 1)
         rows_buf[layer, me] = rows_out[layer]
         if layer == 0:
             wait_all(info_buf, got.at[1], n - 1)
@@ -457,7 +459,6 @@
     last = 2 + layers
     scaled_out[...] = to_rows(weight * potential)
     to_all(scaled_out, scaled_buf, last)
-    halo.send(layers + 1)
     scaled_buf[me] = scaled_out[...]
     wait_all(scaled_buf, got.at[last], n - 1)
     halo.forward(layers)

time: 144 us -> 152 us (1.056)
  Pallas kernels: 132 us -> 140 us
    pallas_call x1, Pallas kernels: 50.8 us -> 57.5 us  [potential_of(): pl.pallas_call(functools.partial(potential_kernel, shape, layers), out_sh...]
where the time goes in v5:
time: 152 us; the launch traced here: 151 us
  Pallas kernels  140 us (92%)
  local copies, waits for them, and re-layouts  5.56 us (4%)
  other arithmetic  3.67 us (2%)
  between operations  2.13 us (1%)
    pallas_call x1, Pallas kernels, halo_of(): pl.pallas_call(functools.partial(halo_kernel, shape), out_shape=(jax.Shap...  57.6 us
    pallas_call x1, Pallas kernels, potential_of(): pl.pallas_call(functools.partial(potential_kernel, shape, layers), out_sh...  57.5 us
    pallas_call x1, Pallas kernels, fock_of(): pl.pallas_call(fock_kernel, out_shape=jax.ShapeDtypeStruct((owned, column...  17.9 us
    pallas_call x1, Pallas kernels, psi_and_density(): pl.pallas_call(psi_kernel, out_shape=(jax.ShapeDtypeStruct((count, points...  6.57 us
    unnamed x19, local copies, waits for them, and re-layouts  4.37 us

profile of v5, /device:TPU:4, one launch (start us, length us, event | category | flops | bytes accessed | tf_op | source)
XLA Modules:
  0.0 150.9 jit_solution(10447358700171262940)
XLA Ops:
  0.6 1.2 slice.13
  1.8 2.0 %fusion.8 = (s32[]{:T(128)}, s32[256]{0:T(256)S(1)}) fusion(s32[256]{0:T(256)} %param.14, s32[]{:T(128)} %bitcast.4), kind=kLoop, calls=%fused_computation.26 | loop fusion | flops 3839 | bytes 2056 | tf_op jit(solution)/shard_map/reduce_min | solution.py:606
  5.1 0.7 broadcast_subtract_fusion
  5.8 0.8 select_reduce_fusion
  6.6 0.1 broadcast_select_fusion.info
  6.7 0.8 copy.18
  7.5 0.1 fusion.hot
  7.6 1.1 copy.17
  8.7 0.0 copy-start
  8.7 1.9 %copy-done = bf16[1536,1024]{1,0:T(8,128)(2,1)S(1)} copy-done((bf16[1536,1024]{1,0:T(8,128)(2,1)S(1)}, bf16[1536,1024]{1,0:T(8,128)(2,1)}, u32[]{:S(2)}) %copy-start) | copy-done | bytes 3145752
  10.6 0.0 copy-start.1
  10.6 57.6 %halo_of.1 = (bf16[1536,1024]{1,0:T(8,128)(2,1)S(1)}, bf16[1536,1024]{1,0:T(8,128)(2,1)S(1)}, bf16[3,4,2,512,128]{4,3,2,1,0:T(8,128)(2,1)S(1)}, s32[3,8,128]{2,1,0:T(8,128)S(1)}, bf16[2,768,1024]{2,1,0:T(8,128)(2,1)}) custom-call(bf16[1536,1024]{1,0:T(8,128)(2,1)S(1)} %copy-done, bf16[2,512,128]{2,1,0:T(8,128)(2,1)S(1)} %bitcast.16, s32[8,128]{1,0:T(8,128)S(1)} %pad.4.names), custom_call_target="tpu_custom_call" | custom-call | tf_op jit(solution)/shard_map/halo_of/pallas_call | solution.py:231
  68.2 0.0 copy-done.1
  68.2 0.0 copy-start.2
  68.2 0.0 copy-start.3
  68.2 0.0 copy-start.4
  68.3 0.0 copy-start.5
  68.3 0.0 copy-start.6
  68.3 0.0 copy-start.7
  68.3 6.6 %psi_and_density.1 = (bf16[8,128,1024]{2,1,0:T(8,128)(2,1)S(1)}, f32[8,128]{1,0:T(8,128)S(1)}) custom-call(s32[8,4]{1,0:T(8,128)S(1)} %subtract_add_fusion.lists, bf16[3,8,512,128]{3,2,1,0:T(8,128)(2,1)S(1)} %bitcast.14, bf16[1536,1024]{1,0:T(8,128)(2,1)S(1)} %get-tuple-element.14.below, bf16[1536,1024]{1,0:T(8,128)(2,1)S(1)} %copy-done.1, ...), custom_call_target="tpu_custom_call" | custom-call | flops 1073741824 | bytes 12582912 | tf_op jit(solution)/shard_map/psi_and_density/pallas_call | solution.py:321
  74.9 0.0 copy-done.2
  74.9 0.0 copy-done.3
  74.9 0.0 copy-done.4
  74.9 0.0 copy-done.5
  74.9 0.0 copy-done.6
  74.9 0.0 copy-done.7
  74.9 57.5 %potential_of.1 = (f32[2,128]{1,0:T(2,128)S(1)}, f32[12,2,128]{2,1,0:T(2,128)S(1)}, bf16[8,128,1024]{2,1,0:T(8,128)(2,1)S(1)}, bf16[8,128,1024]{2,1,0:T(8,128)(2,1)S(1)}, bf16[2,4,128,1024]{3,2,1,0:T(8,128)(2,1)}) custom-call(bf16[8,128,1024]{2,1,0:T(8,128)(2,1)S(1)} %get-tuple-element.16.psi.mid, f32[4,2,128]{2,1,0:T(2,128)S(1)} %bitcast.20, ...), custom_call_target="tpu_custom_call" | custom-call | flops 20000000000 | bytes 4000000 | tf_op jit(solution)/shard_map/potential_of/pallas_call | solution.py:483
  132.5 17.9 %fock_of.1 = f32[1536,1024]{1,0:T(8,128)} custom-call(s32[24,4]{1,0:T(8,128)S(1)} %subtract_bitcast_fusion.lists, bf16[3,8,512,128]{3,2,1,0:T(8,128)(2,1)S(1)} %bitcast.15, f32[24,128]{1,0:T(8,128)S(1)} %bitcast.17, bf16[8,128,1024]{2,1,0:T(8,128)(2,1)S(1)} %get-tuple-element.19.low, bf16[8,128,1024]{2,1,0:T(8,128)(2,1)S(1)} %get-tuple-element.16.psi.mid, ...), custom_call_target="tpu_custom_call" | custom-call | tf_op jit(solution)/shard_map/fock_of/pallas_call | solution.py:556
  150.3 0.6 copy.24
  (7 shorter events, 0.1 us)
Async XLA Ops:
  8.7 1.9 %copy-start = (bf16[1536,1024]{1,0:T(8,128)(2,1)S(1)}, bf16[1536,1024]{1,0:T(8,128)(2,1)}, u32[]{:S(2)}) copy-start(bf16[1536,1024]{1,0:T(8,128)(2,1)} %own.3) | copy-start | bytes 9437188
  10.6 57.6 %copy-start.1 = (bf16[1536,1024]{1,0:T(8,128)(2,1)S(1)}, bf16[1536,1024]{1,0:T(8,128)(2,1)}, u32[]{:S(2)}) copy-start(bf16[1536,1024]{1,0:T(8,128)(2,1)} %own.3) | copy-start | bytes 9437188
  68.2 6.6 %copy-start.2 = (f32[256]{0:T(256)S(1)}, f32[256]{0:T(256)}, u32[]{:S(2)}) copy-start(f32[256]{0:T(256)} %param.13) | copy-start | bytes 3076
  68.2 6.6 %copy-start.3 = (bf16[2,256,256]{2,1,0:T(8,128)(2,1)S(1)}, bf16[2,256,256]{2,1,0:T(8,128)(2,1)}, u32[]{:S(2)}) copy-start(bf16[2,256,256]{2,1,0:T(8,128)(2,1)} %mw.1) | copy-start | bytes 786436
  68.2 6.6 %copy-start.4 = (bf16[2,256,256]{2,1,0:T(8,128)(2,1)S(1)}, bf16[2,256,256]{2,1,0:T(8,128)(2,1)}, u32[]{:S(2)}) copy-start(bf16[2,256,256]{2,1,0:T(8,128)(2,1)} %aw.1) | copy-start | bytes 786436
  68.3 6.6 %copy-start.5 = (f32[256]{0:T(256)S(1)}, f32[256]{0:T(256)}, u32[]{:S(2)}) copy-start(f32[256]{0:T(256)} %param.15) | copy-start | bytes 3076
  68.3 6.6 %copy-start.6 = (f32[256]{0:T(256)S(1)}, f32[256]{0:T(256)}, u32[]{:S(2)}) copy-start(f32[256]{0:T(256)} %param.16) | copy-start | bytes 3076
  68.3 6.6 %copy-start.7 = (f32[256]{0:T(256)S(1)}, f32[256]{0:T(256)}, u32[]{:S(2)}) copy-start(f32[256]{0:T(256)} %param.19) | copy-start | bytes 3076
